TPU v7x, 32 devices: a whole 2x2x4 slice. The times are simulated.
32 devices in a mesh: row: 8 (over z, x), col: 4 (over y, core).
Axes of the slice: x: 2, y: 2, z: 4, core: 2. Of those that a mesh axis runs over, the one named last changes fastest.
Arguments:
- tokens: bfloat16 [64, 12288], P('row', 'col'), may hold values from -6 to 6
- past_tokens: bfloat16 [64, 12288], P('row', 'col'), may hold values from -6 to 6
- out_grad: bfloat16 [64, 12288], P('row', 'col'), may hold values from -3 to 3
- w_in: bfloat16 [12288, 24576], P('col', 'row'), may hold values from -0.0546875 to 0.0546875
- w_out: bfloat16 [24576, 12288], P('row', 'col'), may hold values from -0.0390625 to 0.0390625
Outputs:
- layer_out: bfloat16 [64, 12288], P('row', 'col')
- input_grad: bfloat16 [64, 12288], P('row', 'col')
- grad_w_in: bfloat16 [12288, 24576], P('col', 'row')
- grad_w_out: bfloat16 [24576, 12288], P('row', 'col')
All inputs are finite; a program needn't handle non-finite values.
Results may differ from a plain program's by a relative error of at most 0.005.
Values may be sent and summed in bfloat16 or wider, within the bound.
No kernel may reach another device: no remote copies, remote signals or barrier semaphores. Data moves between devices by JAX's collectives and lax.ppermute only.
A program may use at most 128 MiB of HBM per device.

v0:
```python
import jax
import jax.numpy as jnp
from jax import lax
from jax.sharding import PartitionSpec as P


def gelu_parts(pre):
    cdf = 0.5 * (1.0 + jax.scipy.special.erf(pre * 0.7071067811865476))
    slope = cdf + pre * jnp.exp(-0.5 * pre * pre) * 0.3989422804014327
    return (pre * cdf, slope)


def local(tokens, past_tokens, out_grad, w_in, w_out):
    pre_part = jnp.dot(
        lax.all_gather(tokens, "row", axis=0, tiled=True), w_in, preferred_element_type=jnp.float32
    )
    pre_share = lax.psum_scatter(pre_part, "col", scatter_dimension=0, tiled=True)
    hidden_share = gelu_parts(pre_share)[0].astype(jnp.bfloat16)
    hidden_all = lax.all_gather(hidden_share, "col", axis=0, tiled=True)
    block = hidden_all
    layer_out = lax.psum_scatter(
        jnp.dot(block, w_out, preferred_element_type=jnp.float32),
        "row",
        scatter_dimension=0,
        tiled=True,
    ).astype(jnp.bfloat16)
    past_all, grad_all = (
        lax.all_gather(past_tokens, "row", axis=0, tiled=True),
        lax.all_gather(out_grad, "row", axis=0, tiled=True),
    )
    past_part = jnp.dot(past_all, w_in, preferred_element_type=jnp.float32)
    back_part = lax.dot_general(
        grad_all, w_out, (((1,), (1,)), ((), ())), preferred_element_type=jnp.float32
    )
    past_share, back_share = (
        lax.psum_scatter(past_part, "col", scatter_dimension=0, tiled=True),
        lax.psum_scatter(back_part, "col", scatter_dimension=0, tiled=True),
    )
    act_share, slope = gelu_parts(past_share)
    act_local = act_share.astype(jnp.bfloat16)
    grad_local = (back_share * slope).astype(jnp.bfloat16)
    act_all, hidden_grad = (
        lax.all_gather(act_local, "col", axis=0, tiled=True),
        lax.all_gather(grad_local, "col", axis=0, tiled=True),
    )
    grad_w_out = lax.dot_general(
        act_all, grad_all, (((0,), (0,)), ((), ())), preferred_element_type=jnp.float32
    ).astype(jnp.bfloat16)
    grad_w_in = lax.dot_general(
        past_all, hidden_grad, (((0,), (0,)), ((), ())), preferred_element_type=jnp.float32
    ).astype(jnp.bfloat16)
    block = hidden_grad
    input_grad = lax.psum_scatter(
        lax.dot_general(block, w_in, (((1,), (1,)), ((), ())), preferred_element_type=jnp.float32),
        "row",
        scatter_dimension=0,
        tiled=True,
    ).astype(jnp.bfloat16)
    return (layer_out, input_grad, grad_w_in, grad_w_out)


def solution(mesh):
    in_specs = (P("row", "col"), P("row", "col"), P("row", "col"), P("col", "row"), P("row", "col"))
    out_specs = (P("row", "col"), P("row", "col"), P("col", "row"), P("row", "col"))
    return jax.shard_map(local, mesh=mesh, in_specs=in_specs, out_specs=out_specs, check_vma=False)
```

profile of v0, /device:TPU:0, one launch (start us, length us, event | category | flops | bytes accessed | tf_op | source)
XLA Modules:
  0.0 301.0 jit_solution(17160969050519650466)
XLA Ops:
  7.2 0.0 reduce-scatter.6.cloned.1.call-start
  7.2 33.0 %all_gather.18 = bf16[64,3072]{1,0:T(8,128)(2,1)S(1)} all-gather(bf16[8,3072]{1,0:T(8,128)(2,1)} %param.5), channel_id=1, replica_groups=mesh['row'=8,'col'=4] {'row'}, dimensions={0}, use_global_device_ids=true | all-gather | bytes 442368 | tf_op jit(solution)/shard_map/all_gather | solution.py:15
  40.2 10.6 %fusion.6 = f32[64,3072]{1,0:T(8,128)} fusion(bf16[64,3072]{1,0:T(8,128)(2,1)S(1)} %all_gather.18, bf16[3072,3072]{1,0:T(8,128)(2,1)} %param.8), kind=kOutput, calls=%fused_computation.12 | convolution fusion | flops 1207959552 | bytes 20054016 | tf_op jit(solution)/shard_map/dot_general | solution.py:14
  50.8 0.0 reduce-scatter.6.cloned.1.call-update
  50.9 0.0 reduce-scatter.10.cloned.1.call-start
  50.9 31.0 %all_gather.20 = bf16[64,3072]{1,0:T(8,128)(2,1)S(1)} all-gather(bf16[8,3072]{1,0:T(8,128)(2,1)S(1)} %copy-done), channel_id=1, replica_groups=mesh['row'=8,'col'=4] {'row'}, dimensions={0}, use_global_device_ids=true | all-gather | bytes 442368 | tf_op jit(solution)/shard_map/all_gather | solution.py:29
  81.9 13.1 %fusion.8 = f32[64,3072]{1,0:T(8,128)} fusion(bf16[64,3072]{1,0:T(8,128)(2,1)S(1)} %all_gather.20, bf16[3072,3072]{1,0:T(8,128)(2,1)} %param.9), kind=kOutput, calls=%fused_computation.14 | convolution fusion | flops 1207959552 | bytes 20054016 | tf_op jit(solution)/shard_map/dot_general | solution.py:32
  95.0 0.0 reduce-scatter.10.cloned.1.call-update
  95.0 0.0 reduce-scatter.12.cloned.1.call-start
  95.0 31.0 %all_gather.21 = bf16[64,3072]{1,0:T(8,128)(2,1)S(1)} all-gather(bf16[8,3072]{1,0:T(8,128)(2,1)S(1)} %copy-done.1), channel_id=1, replica_groups=mesh['row'=8,'col'=4] {'row'}, dimensions={0}, use_global_device_ids=true | all-gather | bytes 442368 | tf_op jit(solution)/shard_map/all_gather | solution.py:28
  126.0 10.6 %fusion.9 = f32[64,3072]{1,0:T(8,128)} fusion(bf16[64,3072]{1,0:T(8,128)(2,1)S(1)} %all_gather.21, bf16[3072,3072]{1,0:T(8,128)(2,1)} %param.8), kind=kOutput, calls=%fused_computation.15 | convolution fusion | flops 1207959552 | bytes 20054016 | tf_op jit(solution)/shard_map/dot_general | solution.py:31
  136.6 0.0 reduce-scatter.12.cloned.1.call-update
  136.7 0.0 reduce-scatter.8.cloned.1.call-start
  136.7 0.0 reduce-scatter.6.cloned.1.call-done
  136.7 1.0 multiply_convert_fusion.1
  137.7 6.7 %all_gather.19 = bf16[64,3072]{1,0:T(8,128)(2,1)S(1)} all-gather(bf16[16,3072]{1,0:T(8,128)(2,1)S(1)} %multiply_convert_fusion.1), channel_id=1, replica_groups=mesh['row'=8,'col'=4] {'col'}, dimensions={0}, use_global_device_ids=true | all-gather | bytes 491520 | tf_op jit(solution)/shard_map/all_gather | solution.py:19
  144.4 10.8 %fusion.7 = f32[64,3072]{1,0:T(8,128)} fusion(bf16[64,3072]{1,0:T(8,128)(2,1)S(1)} %all_gather.19, bf16[3072,3072]{1,0:T(8,128)(2,1)} %param.9), kind=kOutput, calls=%fused_computation.13 | convolution fusion | flops 1207959552 | bytes 20054016 | tf_op jit(solution)/shard_map/dot_general | solution.py:22
  155.2 0.0 reduce-scatter.8.cloned.1.call-update
  155.2 0.0 reduce-scatter.14.cloned.1.call-start
  155.3 0.0 reduce-scatter.10.cloned.1.call-done
  155.3 5.8 %reduce-scatter.12.cloned.1.call-done = f32[16,3072]{1,0:T(8,128)} async-done(((f32[64,3072]{1,0:T(8,128)}), f32[16,3072]{1,0:T(8,128)}) %reduce-scatter.12.cloned.1.call-update) | async-done | bytes 196624 | tf_op jit(solution)/shard_map/reduce_scatter | solution.py:36
  161.1 1.1 multiply_convert_fusion
  162.2 6.1 %all_gather.22 = bf16[64,3072]{1,0:T(8,128)(2,1)S(1)} all-gather(bf16[16,3072]{1,0:T(8,128)(2,1)S(1)} %get-tuple-element.9), channel_id=1, replica_groups=mesh['row'=8,'col'=4] {'col'}, dimensions={0}, use_global_device_ids=true | all-gather | bytes 491520 | tf_op jit(solution)/shard_map/all_gather | solution.py:44
  168.3 13.1 %fusion.10 = f32[64,3072]{1,0:T(8,128)} fusion(bf16[64,3072]{1,0:T(8,128)(2,1)S(1)} %all_gather.22, bf16[3072,3072]{1,0:T(8,128)(2,1)} %param.8), kind=kOutput, calls=%fused_computation.16 | convolution fusion | flops 1207959552 | bytes 20054016 | tf_op jit(solution)/shard_map/dot_general | solution.py:54
  181.5 0.0 reduce-scatter.14.cloned.1.call-update
  181.5 9.5 %convert_bitcast_fusion = bf16[3072,3072]{0,1:T(8,128)(2,1)} fusion(bf16[64,3072]{1,0:T(8,128)(2,1)S(1)} %all_gather.22, bf16[64,3072]{1,0:T(8,128)(2,1)S(1)} %all_gather.21), kind=kOutput, calls=%fused_computation | convolution fusion | flops 1217396736 | bytes 19660800 | tf_op jit(solution)/shard_map/dot_general | solution.py:49
  191.0 24.6 %copy.9 = bf16[3072,3072]{1,0:T(8,128)(2,1)} copy(bf16[3072,3072]{0,1:T(8,128)(2,1)} %convert_bitcast_fusion) | data formatting | bytes 37748736
  215.6 6.7 %all_gather.23 = bf16[64,3072]{1,0:T(8,128)(2,1)S(1)} all-gather(bf16[16,3072]{1,0:T(8,128)(2,1)S(1)} %get-tuple-element.8), channel_id=1, replica_groups=mesh['row'=8,'col'=4] {'col'}, dimensions={0}, use_global_device_ids=true | all-gather | bytes 491520 | tf_op jit(solution)/shard_map/all_gather | solution.py:43
  222.4 9.5 %convolution_convert_fusion = bf16[3072,3072]{1,0:T(8,128)(2,1)} fusion(bf16[64,3072]{1,0:T(8,128)(2,1)S(1)} %all_gather.23, bf16[64,3072]{1,0:T(8,128)(2,1)S(1)} %all_gather.20), kind=kOutput, calls=%fused_computation.1 | convolution fusion | flops 1217396736 | bytes 19660800 | tf_op jit(solution)/shard_map/dot_general | solution.py:46
  231.9 1.5 convert_element_type.25
  233.4 59.5 %reduce-scatter.14.cloned.1.call-done = f32[8,3072]{1,0:T(8,128)} async-done(((f32[64,3072]{1,0:T(8,128)}), f32[8,3072]{1,0:T(8,128)}) %reduce-scatter.14.cloned.1.call-update) | async-done | bytes 98320 | tf_op jit(solution)/shard_map/reduce_scatter | solution.py:53
  292.9 1.5 convert_element_type.27
  (5 shorter events, 0.0 us)
Async XLA Ops:
  7.2 43.8 %copy-start = (bf16[8,3072]{1,0:T(8,128)(2,1)S(1)}, bf16[8,3072]{1,0:T(8,128)(2,1)}, u32[]{:S(2)}) copy-start(bf16[8,3072]{1,0:T(8,128)(2,1)} %param.7) | copy-start | bytes 147460
  7.2 129.6 %reduce-scatter.6.cloned.1.call-start = ((), (), s32[]{:S(2)}) async-start(), calls=%async_computation.5 | async-start | bytes 983040 | tf_op jit(solution)/shard_map/reduce_scatter | solution.py:17
  40.2 54.8 %copy-start.1 = (bf16[8,3072]{1,0:T(8,128)(2,1)S(1)}, bf16[8,3072]{1,0:T(8,128)(2,1)}, u32[]{:S(2)}) copy-start(bf16[8,3072]{1,0:T(8,128)(2,1)} %param.6) | copy-start | bytes 147460
  50.9 104.4 %reduce-scatter.10.cloned.1.call-start = ((), (), s32[]{:S(2)}) async-start(), calls=%async_computation.7 | async-start | bytes 983040 | tf_op jit(solution)/shard_map/reduce_scatter | solution.py:37
  95.0 66.1 %reduce-scatter.12.cloned.1.call-start = ((), (), s32[]{:S(2)}) async-start(), calls=%async_computation.8 | async-start | bytes 983040 | tf_op jit(solution)/shard_map/reduce_scatter | solution.py:36
  136.7 95.2 %reduce-scatter.8.cloned.1.call-start = ((), (), s32[]{:S(2)}) async-start(), calls=%async_computation.6 | async-start | bytes 884736 | tf_op jit(solution)/shard_map/reduce_scatter | solution.py:21
  155.2 137.7 %reduce-scatter.14.cloned.1.call-start = ((), (), s32[]{:S(2)}) async-start(), calls=%async_computation.9 | async-start | bytes 884736 | tf_op jit(solution)/shard_map/reduce_scatter | solution.py:53
Sparse Core Ops, SparseCore 0:
  51.0 24.2 reduce-scatter.5
  95.1 24.2 reduce-scatter.9
  136.8 24.2 reduce-scatter.11
  164.2 63.2 reduce-scatter.7
  230.6 62.2 reduce-scatter.13
where the time goes:
time: 302 us; the launch traced here: 301 us
  blocking collectives  114 us (38%)
  matrix products  77.3 us (26%)
  waiting for transfers between devices  65.4 us (22%)
  local copies, waits for them, and re-layouts  24.6 us (8%)
  between operations  13.8 us (5%)
  other arithmetic  5.13 us (2%)
    reduce_scatter x1, waiting for transfers between devices, local(): lax.psum_scatter(lax.dot_general(block, w_in, (((1,), (1,)), ((), ())), p...  59.5 us
    all_gather x1, blocking collectives, local(): lax.all_gather(tokens, 'row', axis=0, tiled=True)  33 us
    all_gather x1, blocking collectives, local(): lax.all_gather(out_grad, 'row', axis=0, tiled=True)  31 us
    all_gather x1, blocking collectives, local(): lax.all_gather(past_tokens, 'row', axis=0, tiled=True)  31 us
    unnamed x5, local copies, waits for them, and re-layouts  24.6 us
    dot_general x1, matrix products, local(): lax.dot_general(block, w_in, (((1,), (1,)), ((), ())), preferred_element_...  13.1 us
    dot_general x1, matrix products, local(): lax.dot_general(grad_all, w_out, (((1,), (1,)), ((), ())), preferred_elem...  13.1 us
    dot_general x1, matrix products, local(): jnp.dot(block, w_out, preferred_element_type=jnp.float32)  10.8 us
  transfers between devices with their start and end apart: 5, of which 2 were waited for; matrix products, arithmetic and copies ran while one was open for 32% of the time, Pallas kernels for 0%

commit v1 on v0

v1 whole, which is shorter than its diff:
```python
import jax
import jax.numpy as jnp
from jax import lax
from jax.sharding import PartitionSpec as P

BF16, F32 = jnp.bfloat16, jnp.float32


def gelu_parts(pre):
    cdf = 0.5 * (1.0 + jax.scipy.special.erf(pre * 0.7071067811865476))
    slope = cdf + pre * jnp.exp(-0.5 * pre * pre) * 0.3989422804014327
    return (pre * cdf, slope)


def swap(x, axis, bit):
    n = lax.axis_size(axis)
    return lax.ppermute(x, axis, [(i, i ^ bit) for i in range(n)])


def bits(n):
    return [1 << k for k in range(n.bit_length() - 1)]


def gather(x, axis, dim):
    for bit in reversed(bits(lax.axis_size(axis))):
        x = jnp.concatenate([x, swap(x, axis, bit)], axis=dim)
    return x


def scatter(x):
    for bit in bits(lax.axis_size("row")):
        half = x.shape[0] // 2
        got = swap(x[half:].astype(BF16), "row", bit)
        x = x[:half] + got.astype(F32)
    return x


def total(x):
    me = lax.axis_index("col")
    half = x.shape[1] // 2
    keep = (me % 2) * half
    mine = lax.dynamic_slice_in_dim(x, keep, half, 1)
    other = lax.dynamic_slice_in_dim(x, half - keep, half, 1)
    x = mine + swap(other, "col", 1)
    for bit in bits(lax.axis_size("col"))[1:]:
        x = x + swap(x.astype(BF16), "col", bit).astype(F32)
    return x


def whole(x):
    other = swap(x, "col", 1)
    low = lax.axis_index("col") % 2 == 0
    return jnp.concatenate([jnp.where(low, x, other), jnp.where(low, other, x)], axis=1)


def local(tokens, past_tokens, out_grad, w_in, w_out):
    x = gather(jnp.stack([tokens, past_tokens, out_grad]), "row", 1)
    both, grad_all = x[:2], x[2]
    past_all = x[1]
    n = both.shape[1]
    back = lax.dot_general(grad_all, w_out, (((1,), (1,)), ((), ())), preferred_element_type=F32)
    pre = jnp.dot(both.reshape(2 * n, -1), w_in, preferred_element_type=F32).reshape(2, n, -1)
    s = total(jnp.concatenate([pre, back[None]]))
    hidden = gelu_parts(s[0])[0]
    act, slope = gelu_parts(s[1])
    h = whole(jnp.stack([hidden, act, s[2] * slope]).astype(BF16))
    hidden_all, act_all, hidden_grad = h[0], h[1], h[2]
    layer = jnp.dot(hidden_all, w_out, preferred_element_type=F32)
    inp = lax.dot_general(hidden_grad, w_in, (((1,), (1,)), ((), ())), preferred_element_type=F32)
    res = scatter(jnp.concatenate([layer, inp], axis=1)).astype(BF16)
    width = layer.shape[1]
    grad_w_out = lax.dot_general(
        act_all, grad_all, (((0,), (0,)), ((), ())), preferred_element_type=F32
    ).astype(BF16)
    grad_w_in = lax.dot_general(
        past_all, hidden_grad, (((0,), (0,)), ((), ())), preferred_element_type=F32
    ).astype(BF16)
    return (res[:, :width], res[:, width:], grad_w_in, grad_w_out)


def solution(mesh):
    in_specs = (P("row", "col"), P("row", "col"), P("row", "col"), P("col", "row"), P("row", "col"))
    out_specs = (P("row", "col"), P("row", "col"), P("col", "row"), P("row", "col"))
    return jax.shard_map(local, mesh=mesh, in_specs=in_specs, out_specs=out_specs, check_vma=False)
```

time: 302 us -> 134 us (0.44)
  blocking collectives: 114 us -> 0 us
  local copies, waits for them, and re-layouts: 24.6 us -> 0.72 us
  matrix products: 77.3 us -> 55.4 us
  starting transfers between devices: 0.21 us -> 14.7 us
  between operations: 13.8 us -> 0.82 us
  waiting for transfers between devices: 65.4 us -> 56 us
    all_gather x6 -> x0, blocking collectives: 114 us -> none  [the longest x1 33 us: local(): lax.all_gather(tokens, 'row', axis=0, tiled=True)]
    reduce_scatter x5 -> x0, waiting for transfers between devices: 65.3 us -> none  [the longest x1 59.5 us: local(): lax.psum_scatter(lax.dot_general(block, w_in, (((1,), (1,)), ((), ())), p...]
    ppermute x0 -> x9, waiting for transfers between devices: none -> 56 us  [swap(): return lax.ppermute(x, axis, [(i, i ^ bit) for i in range(n)])]
    unnamed x5 -> x14, local copies, waits for them, and re-layouts: 24.6 us -> 0.04 us
    dot_general x4 -> x3, matrix products: 45.3 us -> 26.7 us  [the longest x1 9.66 us: local(): lax.dot_general(hidden_grad, w_in, (((1,), (1,)), ((), ())), preferred_el...]
    ppermute x0 -> x9, starting transfers between devices: none -> 14.7 us  [swap(): return lax.ppermute(x, axis, [(i, i ^ bit) for i in range(n)])]
    convert_element_type x4 -> x2, other arithmetic: 5.13 us -> 1.44 us  [the longest x1 1.42 us: total(): x = x + swap(x.astype(BF16), 'col', bit).astype(F32)]
    dot_general x1, matrix products: 13.1 us -> 9.66 us  [local(): lax.dot_general(grad_all, w_out, (((1,), (1,)), ((), ())), preferred_elem...]
  transfers between devices with their start and end apart: 5 -> 9, of which waited for: 2 -> 7; matrix products, arithmetic and copies ran while one was open for 32% -> 14% of each run, Pallas kernels for 0% -> 0%
where the time goes in v1:
time: 134 us
  waiting for transfers between devices  56 us (42%)
  matrix products  55.4 us (41%)
  starting transfers between devices  14.7 us (11%)
  other arithmetic  6.04 us (5%)
    ppermute x9, waiting for transfers between devices, swap(): return lax.ppermute(x, axis, [(i, i ^ bit) for i in range(n)])  56 us
    ppermute x9, starting transfers between devices, swap(): return lax.ppermute(x, axis, [(i, i ^ bit) for i in range(n)])  14.7 us
    dot_general x1, matrix products, local(): lax.dot_general(grad_all, w_out, (((1,), (1,)), ((), ())), preferred_elem...  9.66 us
    dot_general x1, matrix products, local(): lax.dot_general(hidden_grad, w_in, (((1,), (1,)), ((), ())), preferred_el...  9.66 us
    dot_general x1, matrix products, local(): lax.dot_general(past_all, hidden_grad, (((0,), (0,)), ((), ())), preferre...  9.51 us
    dot_general x1, matrix products, local(): lax.dot_general(act_all, grad_all, (((0,), (0,)), ((), ())), preferred_el...  9.49 us
    dot_general x1, matrix products, local(): jnp.dot(both.reshape(2 * n, -1), w_in, preferred_element_type=F32)  8.97 us
    dot_general x1, matrix products, local(): layer = jnp.dot(hidden_all, w_out, preferred_element_type=F32)  8.1 us
  transfers between devices with their start and end apart: 9, of which 7 were waited for; matrix products, arithmetic and copies ran while one was open for 14% of the time, Pallas kernels for 0%

profile of v1, /device:TPU:0, one launch (start us, length us, event | category | flops | bytes accessed | tf_op | source)
XLA Modules:
  0.0 133.7 jit_solution(12022567733178845245)
XLA Ops:
  0.7 0.9 pad_maximum_fusion.5
  1.6 4.1 %collective-permute-start = (bf16[3,8,3072]{2,1,0:T(8,128)(2,1)S(1)}, bf16[3,8,3072]{2,1,0:T(8,128)(2,1)S(1)}, u32[]{:S(2)}, u32[]{:S(2)}) collective-permute-start(bf16[3,8,3072]{2,1,0:T(8,128)(2,1)S(1)} %pad_maximum_fusion.5), channel_id=1, source_target_pairs={{0,16},{4,20},{8,24},{12,28},{16,0},{20,4},{24,8},{28,12},{1,17},{... | collective-permute-start | bytes 442376 | tf_op jit(solution)/shard_map/ppermute | solution.py:17
  5.7 7.0 %collective-permute-done = bf16[3,8,3072]{2,1,0:T(8,128)(2,1)S(1)} collective-permute-done((bf16[3,8,3072]{2,1,0:T(8,128)(2,1)S(1)}, bf16[3,8,3072]{2,1,0:T(8,128)(2,1)S(1)}, u32[]{:S(2)}, u32[]{:S(2)}) %collective-permute-start) | collective-permute-done | bytes 147488 | tf_op jit(solution)/shard_map/ppermute | solution.py:17
  12.7 0.9 pad_maximum_fusion.4
  13.6 0.8 collective-permute-start.1
  14.4 7.5 %collective-permute-done.1 = bf16[3,16,3072]{2,1,0:T(8,128)(2,1)S(1)} collective-permute-done((bf16[3,16,3072]{2,1,0:T(8,128)(2,1)S(1)}, bf16[3,16,3072]{2,1,0:T(8,128)(2,1)S(1)}, u32[]{:S(2)}, u32[]{:S(2)}) %collective-permute-start.1) | collective-permute-done | bytes 294944 | tf_op jit(solution)/shard_map/ppermute | solution.py:17
  21.8 1.0 pad_maximum_fusion.1
  22.8 1.3 %collective-permute-start.2 = (bf16[3,32,3072]{2,1,0:T(8,128)(2,1)S(1)}, bf16[3,32,3072]{2,1,0:T(8,128)(2,1)S(1)}, u32[]{:S(2)}, u32[]{:S(2)}) collective-permute-start(bf16[3,32,3072]{2,1,0:T(8,128)(2,1)S(1)} %pad_maximum_fusion.1), channel_id=1, source_target_pairs={{0,4},{4,0},{8,12},{12,8},{16,20},{20,16},{24,28},{28,24},{1,5},{5... | collective-permute-start | bytes 1769480 | tf_op jit(solution)/shard_map/ppermute | solution.py:17
  24.2 12.4 %collective-permute-done.2 = bf16[3,32,3072]{2,1,0:T(8,128)(2,1)S(1)} collective-permute-done((bf16[3,32,3072]{2,1,0:T(8,128)(2,1)S(1)}, bf16[3,32,3072]{2,1,0:T(8,128)(2,1)S(1)}, u32[]{:S(2)}, u32[]{:S(2)}) %collective-permute-start.2) | collective-permute-done | bytes 589856 | tf_op jit(solution)/shard_map/ppermute | solution.py:17
  36.5 9.7 %convolution_bitcast_fusion = f32[1,64,3072]{2,1,0:T(8,128)S(1)} fusion(bf16[3072,3072]{1,0:T(8,128)(2,1)} %param.9, bf16[3,32,3072]{2,1,0:T(8,128)(2,1)S(1)} %collective-permute-done.2, bf16[3,16,3072]{2,1,0:T(8,128)(2,1)S(1)} %collective-permute-done.1, bf16[3,8,3072]{2,1,0:T(8,128)(2,1)S(1)} %collective-permute-done, ...), kind=kOutput, calls=%fused_computation.4 | convolution fusion | flops 1210318848 | bytes 20840448 | tf_op jit(solution)/shard_map/dot_general | solution.py:61
  46.2 9.0 %fusion = f32[2,64,3072]{2,1,0:T(8,128)S(1)} fusion(bf16[3072,3072]{1,0:T(8,128)(2,1)} %param.8, bf16[3,32,3072]{2,1,0:T(8,128)(2,1)S(1)} %collective-permute-done.2, bf16[3,16,3072]{2,1,0:T(8,128)(2,1)S(1)} %collective-permute-done.1, bf16[3,8,3072]{2,1,0:T(8,128)(2,1)S(1)} %collective-permute-done, bf16[1,8,3072]{2,1,0:T(8,128)(2,1)S(1)} %bitcast.32, ...), kind=kOutput, calls=%fused_computation | convolution fusion | flops 2422996992 | bytes 21626880 | tf_op jit(solution)/shard_map/dot_general | solution.py:62
  55.2 1.1 fusion.2
  56.3 3.2 %collective-permute-done.3 = f32[3,32,3072]{2,1,0:T(8,128)} collective-permute-done((f32[3,32,3072]{2,1,0:T(8,128)}, f32[3,32,3072]{2,1,0:T(8,128)}, u32[]{:S(2)}, u32[]{:S(2)}) %collective-permute-start.3) | collective-permute-done | bytes 1179680 | tf_op jit(solution)/shard_map/ppermute | solution.py:17
  59.5 1.4 %fusion.52 = (bf16[3,32,3072]{2,1,0:T(8,128)(2,1)S(1)}, f32[3,32,3072]{2,1,0:T(8,128)S(1)}) fusion(f32[3,32,3072]{2,1,0:T(8,128)} %collective-permute-done.3, s32[]{:T(128)S(6)} %select_n.29, f32[1,64,3072]{2,1,0:T(8,128)S(1)} %convolution_bitcast_fusion, f32[2,64,3072]{2,1,0:T(8,128)S(1)} %fusion), kind=kLoop, calls=%fused_computation.80 | loop fusion | flops 884736 | bytes 5308420 | tf_op jit(solution)/shard_map/convert_element_type | solution.py:46
  60.9 1.3 %collective-permute-start.4 = (bf16[3,32,3072]{2,1,0:T(8,128)(2,1)S(1)}, bf16[3,32,3072]{2,1,0:T(8,128)(2,1)S(1)}, u32[]{:S(2)}, u32[]{:S(2)}) collective-permute-start(bf16[3,32,3072]{2,1,0:T(8,128)(2,1)S(1)} %get-tuple-element.4), channel_id=1, source_target_pairs={{0,2},{1,3},{2,0},{3,1},{4,6},{5,7},{6,4},{7,5},{8,10},{9,11},{10,... | collective-permute-start | bytes 1769480 | tf_op jit(solution)/shard_map/ppermute | solution.py:17
  62.2 14.1 %collective-permute-done.4 = bf16[3,32,3072]{2,1,0:T(8,128)(2,1)S(1)} collective-permute-done((bf16[3,32,3072]{2,1,0:T(8,128)(2,1)S(1)}, bf16[3,32,3072]{2,1,0:T(8,128)(2,1)S(1)}, u32[]{:S(2)}, u32[]{:S(2)}) %collective-permute-start.4) | collective-permute-done | bytes 589856 | tf_op jit(solution)/shard_map/ppermute | solution.py:17
  76.3 0.1 convert_add_fusion
  76.5 0.3 multiply_convert_fusion.1
  76.7 0.1 pad_maximum_fusion.2
  76.8 0.1 collective-permute-start.5
  76.9 2.0 %collective-permute-done.5 = bf16[3,32,3072]{2,1,0:T(8,128)(2,1)S(1)} collective-permute-done((bf16[3,32,3072]{2,1,0:T(8,128)(2,1)S(1)}, bf16[3,32,3072]{2,1,0:T(8,128)(2,1)S(1)}, u32[]{:S(2)}, u32[]{:S(2)}) %collective-permute-start.5) | collective-permute-done | bytes 589856 | tf_op jit(solution)/shard_map/ppermute | solution.py:17
  78.9 0.1 broadcast_select_fusion
  79.0 8.1 %fusion.29 = f32[64,3072]{1,0:T(8,128)S(1)} fusion(bf16[3072,3072]{1,0:T(8,128)(2,1)} %param.9, bf16[3,32,3072]{2,1,0:T(8,128)(2,1)S(1)} %get-tuple-element.7, bf16[3,32,3072]{2,1,0:T(8,128)(2,1)S(1)} %get-tuple-element.6), kind=kOutput, calls=%fused_computation.49 | convolution fusion | flops 1208745984 | bytes 20840448 | tf_op jit(solution)/shard_map/dot_general | solution.py:68
  87.1 9.7 %fusion.50 = f32[64,3072]{1,0:T(8,128)S(1)} fusion(bf16[3072,3072]{1,0:T(8,128)(2,1)} %param.8, bf16[3,32,3072]{2,1,0:T(8,128)(2,1)S(1)} %get-tuple-element.7, bf16[3,32,3072]{2,1,0:T(8,128)(2,1)S(1)} %get-tuple-element.6), kind=kOutput, calls=%fused_computation.79 | convolution fusion | flops 1208745984 | bytes 20840448 | tf_op jit(solution)/shard_map/dot_general | solution.py:69
  96.9 1.3 collective-permute-start.6
  98.2 9.9 %collective-permute-done.6 = bf16[32,6144]{1,0:T(8,128)(2,1)S(1)} collective-permute-done((bf16[32,6144]{1,0:T(8,128)(2,1)S(1)}, bf16[32,6144]{1,0:T(8,128)(2,1)S(1)}, u32[]{:S(2)}, u32[]{:S(2)}) %collective-permute-start.6) | collective-permute-done | bytes 393248 | tf_op jit(solution)/shard_map/ppermute | solution.py:17
  108.1 0.1 fusion.17
  108.2 2.3 %collective-permute-start.7 = (bf16[16,6144]{1,0:T(8,128)(2,1)S(1)}, bf16[16,6144]{1,0:T(8,128)(2,1)S(1)}, u32[]{:S(2)}, u32[]{:S(2)}) collective-permute-start(bf16[16,6144]{1,0:T(8,128)(2,1)S(1)} %slice.131), channel_id=1, source_target_pairs={{0,8},{4,12},{8,0},{12,4},{16,24},{20,28},{24,16},{28,20},{1,9},{5... | collective-permute-start | bytes 589832 | tf_op jit(solution)/shard_map/ppermute | solution.py:17
  110.5 9.5 %convolution_convert_fusion.1 = bf16[3072,3072]{1,0:T(8,128)(2,1)} fusion(bf16[3,32,3072]{2,1,0:T(8,128)(2,1)S(1)} %collective-permute-done.2, bf16[3,16,3072]{2,1,0:T(8,128)(2,1)S(1)} %copy-done.1, bf16[3,8,3072]{2,1,0:T(8,128)(2,1)S(1)} %collective-permute-done, bf16[1,8,3072]{2,1,0:T(8,128)(2,1)S(1)} %bitcast.33, bf16[1,8,3072]{2,1,0:T(8,128)(2,1)S(1)} %bitcast.40, ...), kind=kOutput, calls=%fused_computation.3 | convolution fusion | flops 1220542464 | bytes 21233664 | tf_op jit(solution)/shard_map/dot_general | solution.py:75
  120.1 3.4 %collective-permute-start.8 = (bf16[8,6144]{1,0:T(8,128)(2,1)S(1)}, bf16[8,6144]{1,0:T(8,128)(2,1)S(1)}, u32[]{:S(2)}, u32[]{:S(2)}) collective-permute-start(bf16[8,6144]{1,0:T(8,128)(2,1)S(1)} %slice.132), channel_id=1, source_target_pairs={{0,16},{4,20},{8,24},{12,28},{16,0},{20,4},{24,8},{28,12},{1,17},{... | collective-permute-start | bytes 294920 | tf_op jit(solution)/shard_map/ppermute | solution.py:17
  123.5 9.5 %convolution_convert_fusion = bf16[3072,3072]{1,0:T(8,128)(2,1)} fusion(bf16[3,32,3072]{2,1,0:T(8,128)(2,1)S(1)} %get-tuple-element.6, bf16[3,32,3072]{2,1,0:T(8,128)(2,1)S(1)} %get-tuple-element.7, bf16[3,32,3072]{2,1,0:T(8,128)(2,1)S(1)} %collective-permute-done.2, bf16[3,16,3072]{2,1,0:T(8,128)(2,1)S(1)} %copy-done.1, ...), kind=kOutput, calls=%fused_computation.2 | convolution fusion | flops 1220542464 | bytes 21233664 | tf_op jit(solution)/shard_map/dot_general | solution.py:72
  133.1 0.6 fusion.54
  (22 shorter events, 0.2 us)
Async XLA Ops:
  0.6 35.9 %copy-start.2 = (bf16[8,3072]{1,0:T(8,128)(2,1)S(1)}, bf16[8,3072]{1,0:T(8,128)(2,1)}, u32[]{:S(2)}) copy-start(bf16[8,3072]{1,0:T(8,128)(2,1)} %param.7) | copy-start | bytes 147460
  0.6 35.9 %copy-start.3 = (bf16[8,3072]{1,0:T(8,128)(2,1)S(1)}, bf16[8,3072]{1,0:T(8,128)(2,1)}, u32[]{:S(2)}) copy-start(bf16[8,3072]{1,0:T(8,128)(2,1)} %param.6) | copy-start | bytes 147460
  0.7 35.9 %copy-start.5 = (bf16[8,3072]{1,0:T(8,128)(2,1)S(1)}, bf16[8,3072]{1,0:T(8,128)(2,1)}, u32[]{:S(2)}) copy-start(bf16[8,3072]{1,0:T(8,128)(2,1)} %param.5) | copy-start | bytes 147460
  1.6 11.1 %collective-permute-start = (bf16[3,8,3072]{2,1,0:T(8,128)(2,1)S(1)}, bf16[3,8,3072]{2,1,0:T(8,128)(2,1)S(1)}, u32[]{:S(2)}, u32[]{:S(2)}) collective-permute-start(bf16[3,8,3072]{2,1,0:T(8,128)(2,1)S(1)} %pad_maximum_fusion.5), channel_id=1, source_target_pairs={{0,16},{4,20},{8,24},{12,28},{16,0},{20,4},{24,8},{28,12},{1,17},{... | collective-permute-start | bytes 442376 | tf_op jit(solution)/shard_map/ppermute | solution.py:17
  13.6 8.2 %collective-permute-start.1 = (bf16[3,16,3072]{2,1,0:T(8,128)(2,1)S(1)}, bf16[3,16,3072]{2,1,0:T(8,128)(2,1)S(1)}, u32[]{:S(2)}, u32[]{:S(2)}) collective-permute-start(bf16[3,16,3072]{2,1,0:T(8,128)(2,1)S(1)} %pad_maximum_fusion.4), channel_id=1, source_target_pairs={{0,8},{4,12},{8,0},{12,4},{16,24},{20,28},{24,16},{28,20},{1,9},{5... | collective-permute-start | bytes 884744 | tf_op jit(solution)/shard_map/ppermute | solution.py:17
  21.8 24.4 %copy-start = (bf16[3,16,3072]{2,1,0:T(8,128)(2,1)}, bf16[3,16,3072]{2,1,0:T(8,128)(2,1)S(1)}, u32[]{:S(2)}) copy-start(bf16[3,16,3072]{2,1,0:T(8,128)(2,1)S(1)} %collective-permute-done.1) | copy-start | bytes 884740
  22.8 13.7 %collective-permute-start.2 = (bf16[3,32,3072]{2,1,0:T(8,128)(2,1)S(1)}, bf16[3,32,3072]{2,1,0:T(8,128)(2,1)S(1)}, u32[]{:S(2)}, u32[]{:S(2)}) collective-permute-start(bf16[3,32,3072]{2,1,0:T(8,128)(2,1)S(1)} %pad_maximum_fusion.1), channel_id=1, source_target_pairs={{0,4},{4,0},{8,12},{12,8},{16,20},{20,16},{24,28},{28,24},{1,5},{5... | collective-permute-start | bytes 1769480 | tf_op jit(solution)/shard_map/ppermute | solution.py:17
  56.3 3.2 %collective-permute-start.3 = (f32[3,32,3072]{2,1,0:T(8,128)}, f32[3,32,3072]{2,1,0:T(8,128)}, u32[]{:S(2)}, u32[]{:S(2)}) collective-permute-start(f32[3,32,3072]{2,1,0:T(8,128)} %fusion.2), channel_id=1, source_target_pairs={{0,1},{1,0},{2,3},{3,2},{4,5},{5,4},{6,7},{7,6},{8,9},{9,8},{10,11... | collective-permute-start | bytes 3538952 | tf_op jit(solution)/shard_map/ppermute | solution.py:17
  60.9 15.4 %collective-permute-start.4 = (bf16[3,32,3072]{2,1,0:T(8,128)(2,1)S(1)}, bf16[3,32,3072]{2,1,0:T(8,128)(2,1)S(1)}, u32[]{:S(2)}, u32[]{:S(2)}) collective-permute-start(bf16[3,32,3072]{2,1,0:T(8,128)(2,1)S(1)} %get-tuple-element.4), channel_id=1, source_target_pairs={{0,2},{1,3},{2,0},{3,1},{4,6},{5,7},{6,4},{7,5},{8,10},{9,11},{10,... | collective-permute-start | bytes 1769480 | tf_op jit(solution)/shard_map/ppermute | solution.py:17
  76.8 2.1 %collective-permute-start.5 = (bf16[3,32,3072]{2,1,0:T(8,128)(2,1)S(1)}, bf16[3,32,3072]{2,1,0:T(8,128)(2,1)S(1)}, u32[]{:S(2)}, u32[]{:S(2)}) collective-permute-start(bf16[3,32,3072]{2,1,0:T(8,128)(2,1)S(1)} %pad_maximum_fusion.2), channel_id=1, source_target_pairs={{0,1},{1,0},{2,3},{3,2},{4,5},{5,4},{6,7},{7,6},{8,9},{9,8},{10,11... | collective-permute-start | bytes 1769480 | tf_op jit(solution)/shard_map/ppermute | solution.py:17
  96.8 13.7 %copy-start.1 = (bf16[3,16,3072]{2,1,0:T(8,128)(2,1)S(1)}, bf16[3,16,3072]{2,1,0:T(8,128)(2,1)}, u32[]{:S(2)}) copy-start(bf16[3,16,3072]{2,1,0:T(8,128)(2,1)} %copy-done) | copy-start | bytes 884740
  96.8 13.7 %copy-start.4 = (bf16[8,3072]{1,0:T(8,128)(2,1)S(1)}, bf16[8,3072]{1,0:T(8,128)(2,1)}, u32[]{:S(2)}) copy-start(bf16[8,3072]{1,0:T(8,128)(2,1)} %param.6) | copy-start | bytes 147460
  96.8 13.7 %copy-start.6 = (bf16[8,3072]{1,0:T(8,128)(2,1)S(1)}, bf16[8,3072]{1,0:T(8,128)(2,1)}, u32[]{:S(2)}) copy-start(bf16[8,3072]{1,0:T(8,128)(2,1)} %param.5) | copy-start | bytes 147460
  96.9 11.2 %collective-permute-start.6 = (bf16[32,6144]{1,0:T(8,128)(2,1)S(1)}, bf16[32,6144]{1,0:T(8,128)(2,1)S(1)}, u32[]{:S(2)}, u32[]{:S(2)}) collective-permute-start(bf16[32,6144]{1,0:T(8,128)(2,1)S(1)} %fusion.18), channel_id=1, source_target_pairs={{0,4},{4,0},{8,12},{12,8},{16,20},{20,16},{24,28},{28,24},{1,5},{5... | collective-permute-start | bytes 1179656 | tf_op jit(solution)/shard_map/ppermute | solution.py:17
  108.2 11.8 %collective-permute-start.7 = (bf16[16,6144]{1,0:T(8,128)(2,1)S(1)}, bf16[16,6144]{1,0:T(8,128)(2,1)S(1)}, u32[]{:S(2)}, u32[]{:S(2)}) collective-permute-start(bf16[16,6144]{1,0:T(8,128)(2,1)S(1)} %slice.131), channel_id=1, source_target_pairs={{0,8},{4,12},{8,0},{12,4},{16,24},{20,28},{24,16},{28,20},{1,9},{5... | collective-permute-start | bytes 589832 | tf_op jit(solution)/shard_map/ppermute | solution.py:17
  120.1 12.9 %collective-permute-start.8 = (bf16[8,6144]{1,0:T(8,128)(2,1)S(1)}, bf16[8,6144]{1,0:T(8,128)(2,1)S(1)}, u32[]{:S(2)}, u32[]{:S(2)}) collective-permute-start(bf16[8,6144]{1,0:T(8,128)(2,1)S(1)} %slice.132), channel_id=1, source_target_pairs={{0,16},{4,20},{8,24},{12,28},{16,0},{20,4},{24,8},{28,12},{1,17},{... | collective-permute-start | bytes 294920 | tf_op jit(solution)/shard_map/ppermute | solution.py:17

commit v2 on v1

v2 whole, which is shorter than its diff:
```python
import jax
import jax.numpy as jnp
from jax import lax
from jax.experimental import pallas as pl
from jax.experimental.pallas import tpu as pltpu
from jax.sharding import PartitionSpec as P


BF16, F32 = jnp.bfloat16, jnp.float32
MIB = 1 << 20
FLOPS = 128
NN, NT, TN = ((1,), (0,)), ((1,), (1,)), ((0,), (0,))


def gelu_parts(pre):
    cdf = 0.5 * (1.0 + jax.scipy.special.erf(pre * 0.7071067811865476))
    slope = cdf + pre * jnp.exp(-0.5 * pre * pre) * 0.3989422804014327
    return (pre * cdf, slope)


def swap(x, axis, bit):
    n = lax.axis_size(axis)
    return lax.ppermute(x, axis, [(i, i ^ bit) for i in range(n)])


def bits(n):
    return [1 << k for k in range(n.bit_length() - 1)]


def block_of(n, most):
    return max(b for b in range(128, n + 1, 128) if n % b == 0 and b <= max(most, 128))


def dot(x, y, dims):
    return lax.dot_general(x, y, (dims, ((), ())), preferred_element_type=F32)


def call(kernel, in_specs, out_specs, out_shape, scratch, macs, moved, *args, grant=6, aliases={}, after=None):
    body = kernel
    if after is not None:
        in_specs, args = [*in_specs, pl.BlockSpec(memory_space=pl.ANY)], (*args, after)
        at = len(args) - 1

        def body(*refs):
            kernel(*refs[:at], *refs[at + 1 :])

    return pl.pallas_call(
        body,
        in_specs=in_specs,
        out_specs=out_specs,
        out_shape=out_shape,
        scratch_shapes=scratch,
        input_output_aliases=aliases,
        compiler_params=pltpu.CompilerParams(vmem_limit_bytes=grant * MIB),
        cost_estimate=pl.CostEstimate(flops=FLOPS * macs, bytes_accessed=moved, transcendentals=0),
    )(*args)


VMEM = pl.BlockSpec(memory_space=pltpu.VMEM)
SMEM = pl.BlockSpec(memory_space=pltpu.SMEM)
HBM = pl.BlockSpec(memory_space=pltpu.HBM)


def core():
    return lax.rem(lax.axis_index("col"), 2)


def load(w, after, parts=8):
    rows = w.shape[0] // parts

    def kernel(w_ref, o_ref, sems):
        copies = [
            pltpu.make_async_copy(w_ref.at[pl.ds(i * rows, rows)], o_ref.at[pl.ds(i * rows, rows)], sems.at[i])
            for i in range(parts)
        ]
        for copy in copies:
            copy.start()
        for copy in copies:
            copy.wait()

    return call(
        kernel,
        [HBM],
        VMEM,
        pltpu.VMEM(w.shape, w.dtype),
        [pltpu.SemaphoreType.DMA((parts,))],
        w.size,
        2 * w.size,
        pltpu.with_memory_space_constraint(w, pltpu.HBM),
        grant=2,
        after=after,
    )


def stream(w_ref, held, sems, b, free, body, ahead=3):
    n = w_ref.shape[free] // b

    def part(j):
        return pl.ds(pl.multiple_of(j * b, b), b)

    def copy(j):
        at = (slice(None), part(j)) if free == 1 else (part(j), slice(None))
        return pltpu.make_async_copy(w_ref.at[at], held.at[at], sems.at[j])

    if sems is not None:
        for j in range(min(ahead, n)):
            copy(j).start()

    @pl.loop(0, n)
    def _(j):
        if sems is not None:
            copy(j).wait()

            @pl.when(j + ahead < n)
            def _():
                copy(j + ahead).start()

        body(part(j))


def into(x, y, w, rows, dims, after=None):
    free = 1 - dims[1][0]
    k, n = w.shape[dims[1][0]], w.shape[free]
    h = x.shape[1]
    first, count, groups = rows
    tall = count // groups // 2
    here = after is None
    b = block_of(n, 1024 if here else 512)

    def kernel(core_ref, x_ref, y_ref, w_ref, mine_ref, send_ref, held, *sems):
        one = pl.ds(first, count)
        low = core_ref[0] == 0
        w_from = w_ref if here else held

        def body(part):
            if free == 1:
                left, right = w_from[:h, part], w_from[h:, part]
            else:
                left, right = w_from[part, :h], w_from[part, h:]
            acc = dot(x_ref[one, :], left, dims) + dot(y_ref[one, :], right, dims)
            for g in range(groups):
                at = 2 * g * tall
                lo, hi = acc[at : at + tall], acc[at + tall : at + 2 * tall]
                put = pl.ds(g * tall, tall)
                mine_ref[put, part] = jnp.where(low, lo, hi)
                send_ref[put, part] = jnp.where(low, hi, lo)

        stream(w_ref, held, None if here else sems[0], b, free, body)

    shape = jax.ShapeDtypeStruct((count // 2, n), F32)
    me = jnp.full((1,), core(), jnp.int32)
    space = pltpu.VMEM if here else pltpu.HBM
    return call(
        kernel,
        [SMEM, VMEM, VMEM, VMEM if here else HBM],
        [VMEM, VMEM, VMEM],
        [shape, shape, pltpu.VMEM(w.shape, w.dtype)],
        [] if here else [pltpu.SemaphoreType.DMA((n // b,))],
        k * n,
        2 * k * n,
        me,
        x,
        y,
        pltpu.with_memory_space_constraint(w, space),
        aliases={3: 2} if here else {},
        after=after,
    )


def outof(own, other, w, dims, here, after):
    free = 1 - dims[1][0]
    k, n = w.shape[dims[1][0]], w.shape[free]
    half = own.shape[0]
    b = block_of(n, 1024 if here else 512)

    def kernel(core_ref, own_ref, other_ref, w_ref, keep_ref, send_ref, x_ref, *scratch):
        low = core_ref[0] == 0
        one, two = own_ref[...], other_ref[...]
        x_ref[:half, :] = jnp.where(low, one, two)
        x_ref[half:, :] = jnp.where(low, two, one)
        held, sems = scratch or (w_ref, None)

        def body(part):
            acc = dot(x_ref[...], held[:, part] if free == 1 else held[part, :], dims)
            keep_ref[:, part] = acc[:half]
            send_ref[:, part] = acc[half:].astype(BF16)

        stream(w_ref, held, sems, b, free, body)

    me = jnp.full((1,), core(), jnp.int32)
    scratch = [] if here else [pltpu.VMEM(w.shape, w.dtype), pltpu.SemaphoreType.DMA((n // b,))]
    return call(
        kernel,
        [SMEM, VMEM, VMEM, VMEM if here else HBM],
        [VMEM, VMEM],
        [jax.ShapeDtypeStruct((half, n), F32), jax.ShapeDtypeStruct((half, n), BF16)],
        [pltpu.VMEM((2 * half, k), BF16), *scratch],
        k * n,
        2 * k * n,
        me,
        own,
        other,
        pltpu.with_memory_space_constraint(w, pltpu.VMEM if here else pltpu.HBM),
        grant=6 if here else 26,
        after=after,
    )


def outer(jobs, after):
    blocks, olds = [], []
    for i, (x, _, old, first, rows) in enumerate(jobs):
        b = block_of(rows, 512)
        blocks += [(i, first + j, b) for j in range(0, rows, b)]
        if old is not None:
            olds.append((i, pltpu.with_memory_space_constraint(old, pltpu.HBM)))
    tall = max(b for _, _, b in blocks)
    width = jobs[0][1].shape[1]
    count = len(jobs)

    def kernel(*refs):
        sides = refs[: 2 * count]
        outs = refs[2 * count + len(olds) : 3 * count + len(olds)]
        held, sems = refs[3 * count + len(olds) :]
        copies = []
        for at, (i, row, b) in enumerate(blocks):
            part = pl.ds(row, b)
            space = held.at[at, pl.ds(0, b)]
            space[...] = dot(sides[2 * i][:, part], sides[2 * i + 1][...], TN).astype(BF16)
            copies.append(pltpu.make_async_copy(space, outs[i].at[part], sems.at[at]))
            copies[-1].start()
        for copy in copies:
            copy.wait()

    moved = sum(b for _, _, b in blocks) * width
    return call(
        kernel,
        [VMEM] * (2 * count) + [HBM] * len(olds),
        [HBM] * count,
        [pltpu.HBM((x.shape[1], width), BF16) for x, *_ in jobs],
        [pltpu.VMEM((len(blocks), tall, width), BF16), pltpu.SemaphoreType.DMA((len(blocks),))],
        moved,
        2 * moved,
        *[side for x, y, *_ in jobs for side in (x, y)],
        *[old for _, old in olds],
        grant=20,
        aliases={2 * count + at: i for at, (i, _) in enumerate(olds)},
        after=after,
    )


def gather(left, right):
    all_bits = bits(lax.axis_size("row"))
    one = all_bits[::-1]
    two = all_bits[:1] + all_bits[:0:-1]
    order_one, order_two = [0], [0]
    tall = left.shape[1]
    for a, b in zip(one, two):
        last = right
        from_left, from_right = swap(left, "row", a), swap(right, "row", b)
        left = jnp.concatenate([left, from_left], axis=1)
        right = jnp.concatenate([right, from_right], axis=1)
        order_one += [j ^ a for j in order_one]
        order_two += [j ^ b for j in order_two]
    at = [order_two.index(j) * tall for j in order_one]
    right = jnp.concatenate([right[:, i : i + tall] for i in at], axis=1)
    return left, right, last


def pair_sum(mine, send):
    return mine + swap(send, "col", 1)


def col_send(x):
    return lax.optimization_barrier(x.astype(BF16))


def col_sum(x, sent):
    for bit in bits(lax.axis_size("col"))[1:]:
        x = x + swap(sent, "col", bit).astype(F32)
        sent = x.astype(BF16)
    return x


def in_order(own, other):
    low = core() == 0
    return jnp.concatenate([jnp.where(low, own, other), jnp.where(low, other, own)], axis=0)


def local(tokens, past_tokens, out_grad, w_in, w_out):
    x = lax.optimization_barrier(jnp.stack([tokens, past_tokens, out_grad]))
    width = x.shape[2]
    h = width // 2
    left, right, last = gather(x[:, :, :h], x[:, :, h:])
    n = left.shape[1]
    half = n // 2
    left, right = left.reshape(3 * n, h), right.reshape(3 * n, h)
    mine, send, w_in_here = into(left, right, load(w_in, last), (0, 2 * n, 2), NN)
    pre = pair_sum(mine, send)
    pre_sent = col_send(pre)
    mine, send, w_out_here = into(left, right, w_out, (2 * n, n, 1), NT, pre_sent)
    back = pair_sum(mine, send)
    back_sent = col_send(back)
    pre = col_sum(pre, pre_sent)
    hidden = gelu_parts(pre[:half])[0]
    act, slope = gelu_parts(pre[half:])
    own, slope = lax.optimization_barrier((jnp.concatenate([hidden, act], axis=0).astype(BF16), slope))
    other = swap(own, "col", 1)
    layer = outof(own[:half], other[:half], w_out_here, NN, True, back_sent)
    back = col_sum(back, back_sent)
    own_grad = (back * slope).astype(BF16)
    other_grad = swap(own_grad, "col", 1)
    inp = outof(own_grad, other_grad, w_in_here, NT, True, layer[1])
    past_all = jnp.concatenate([left[n : 2 * n], right[n : 2 * n]], axis=1)
    grad_all = jnp.concatenate([left[2 * n :], right[2 * n :]], axis=1)
    row_bits = bits(lax.axis_size("row"))
    sums = [keep + swap(send, "row", row_bits[0]).astype(F32) for (keep, send) in (layer, inp)]
    act_all, hidden_grad = in_order(own[half:], other[half:]), in_order(own_grad, other_grad)
    units = act_all.shape[1], past_all.shape[1]
    share = units[0] * 2 // 3 // 128 * 128, units[1] // 3 // 128 * 128
    (grad_w_out,) = outer([(act_all, grad_all, None, 0, share[0])], inp[1])
    res = jnp.concatenate(sums, axis=1)
    for i, bit in enumerate(row_bits[1:]):
        m = res.shape[0] // 2
        sent = lax.optimization_barrier(res[m:].astype(BF16))
        if i == 0:
            grad_w_out, grad_w_in = outer(
                [
                    (act_all, grad_all, grad_w_out, share[0], units[0] - share[0]),
                    (past_all, hidden_grad, None, 0, share[1]),
                ],
                sent,
            )
        elif i == 1:
            (grad_w_in,) = outer([(past_all, hidden_grad, grad_w_in, share[1], units[1] - share[1])], sent)
        res = res[:m] + swap(sent, "row", bit).astype(F32)
    res = res.astype(BF16)
    return (res[:, :width], res[:, width:], grad_w_in, grad_w_out)


def solution(mesh):
    in_specs = (P("row", "col"), P("row", "col"), P("row", "col"), P("col", "row"), P("row", "col"))
    out_specs = (P("row", "col"), P("row", "col"), P("col", "row"), P("row", "col"))

    return jax.shard_map(local, mesh=mesh, in_specs=in_specs, out_specs=out_specs, check_vma=False)
```

time: 134 us -> 93.1 us (0.69)
  matrix products: 55.4 us -> 0 us
  Pallas kernels: 0 us -> 45.1 us
  waiting for transfers between devices: 56 us -> 22.7 us
  starting transfers between devices: 14.7 us -> 21.5 us
  other arithmetic: 6.04 us -> 1.88 us
    dot_general x6 -> x0, matrix products: 55.4 us -> none  [the longest x1 9.66 us: local(): lax.dot_general(grad_all, w_out, (((1,), (1,)), ((), ())), preferred_elem...]
    pallas_call x0 -> x8, Pallas kernels: none -> 45.1 us  [call(): pl.pallas_call(body, in_specs=in_specs, out_specs=out_specs, out_shape=ou...]
    ppermute x9 -> x16, waiting for transfers between devices: 56 us -> 22.7 us  [swap(): return lax.ppermute(x, axis, [(i, i ^ bit) for i in range(n)])]
    ppermute x9 -> x16, starting transfers between devices: 14.7 us -> 21.5 us  [swap(): return lax.ppermute(x, axis, [(i, i ^ bit) for i in range(n)])]
    concatenate x3 -> x9, other arithmetic: 2.96 us -> 0.25 us  [the longest x3 0.08 us: gather(): left = jnp.concatenate([left, from_left], axis=1)]
  transfers between devices with their start and end apart: 9 -> 16, of which waited for: 7 -> 8; matrix products, arithmetic and copies ran while one was open for 14% -> 1% of each run, Pallas kernels for 0% -> 45%
where the time goes in v2:
time: 93.1 us; the launch traced here: 92.9 us
  Pallas kernels  45.1 us (48%)
  waiting for transfers between devices  22.7 us (24%)
  starting transfers between devices  21.5 us (23%)
  other arithmetic  1.88 us (2%)
  between operations  0.97 us (1%)
    pallas_call x8, Pallas kernels, call(): pl.pallas_call(body, in_specs=in_specs, out_specs=out_specs, out_shape=ou...  45.1 us
    ppermute x16, waiting for transfers between devices, swap(): return lax.ppermute(x, axis, [(i, i ^ bit) for i in range(n)])  22.7 us
    ppermute x16, starting transfers between devices, swap(): return lax.ppermute(x, axis, [(i, i ^ bit) for i in range(n)])  21.5 us
  transfers between devices with their start and end apart: 16, of which 8 were waited for; matrix products, arithmetic and copies ran while one was open for 1% of the time, Pallas kernels for 45%

profile of v2, /device:TPU:0, one launch (start us, length us, event | category | flops | bytes accessed | tf_op | source)
XLA Modules:
  0.0 92.9 jit_solution(5144936997750994169)
XLA Ops:
  0.6 0.9 pad_maximum_fusion.9
  1.5 4.1 %collective-permute-start = (bf16[3,8,1536]{2,1,0:T(8,128)(2,1)S(1)}, bf16[3,8,1536]{2,1,0:T(8,128)(2,1)S(1)}, u32[]{:S(2)}, u32[]{:S(2)}) collective-permute-start(bf16[3,8,1536]{2,1,0:T(8,128)(2,1)S(1)} %get-tuple-element.51), channel_id=1, source_target_pairs={{0,16},{4,20},{8,24},{12,28},{16,0},{20,4},{24,8},{28,12},{1,17},{... | collective-permute-start | bytes 221192 | tf_op jit(solution)/shard_map/ppermute | solution.py:23
  5.7 1.5 %collective-permute-start.3 = (bf16[3,8,1536]{2,1,0:T(8,128)(2,1)S(1)}, bf16[3,8,1536]{2,1,0:T(8,128)(2,1)S(1)}, u32[]{:S(2)}, u32[]{:S(2)}) collective-permute-start(bf16[3,8,1536]{2,1,0:T(8,128)(2,1)S(1)} %get-tuple-element.49), channel_id=1, source_target_pairs={{0,4},{4,0},{8,12},{12,8},{16,20},{20,16},{24,28},{28,24},{1,5},{5... | collective-permute-start | bytes 221192 | tf_op jit(solution)/shard_map/ppermute | solution.py:23
  7.1 2.4 %collective-permute-done = bf16[3,8,1536]{2,1,0:T(8,128)(2,1)S(1)} collective-permute-done((bf16[3,8,1536]{2,1,0:T(8,128)(2,1)S(1)}, bf16[3,8,1536]{2,1,0:T(8,128)(2,1)S(1)}, u32[]{:S(2)}, u32[]{:S(2)}) %collective-permute-start) | collective-permute-done | bytes 73760 | tf_op jit(solution)/shard_map/ppermute | solution.py:23
  9.6 0.7 collective-permute-start.1
  10.3 3.4 %collective-permute-start.4 = (bf16[3,16,1536]{2,1,0:T(8,128)(2,1)S(1)}, bf16[3,16,1536]{2,1,0:T(8,128)(2,1)S(1)}, u32[]{:S(2)}, u32[]{:S(2)}) collective-permute-start(bf16[3,16,1536]{2,1,0:T(8,128)(2,1)S(1)} %pad_maximum_fusion.11), channel_id=1, source_target_pairs={{0,16},{4,20},{8,24},{12,28},{16,0},{20,4},{24,8},{28,12},{1,17},{... | collective-permute-start | bytes 442376 | tf_op jit(solution)/shard_map/ppermute | solution.py:23
  13.8 3.5 %collective-permute-done.1 = bf16[3,16,1536]{2,1,0:T(8,128)(2,1)S(1)} collective-permute-done((bf16[3,16,1536]{2,1,0:T(8,128)(2,1)S(1)}, bf16[3,16,1536]{2,1,0:T(8,128)(2,1)S(1)}, u32[]{:S(2)}, u32[]{:S(2)}) %collective-permute-start.1) | collective-permute-done | bytes 147488 | tf_op jit(solution)/shard_map/ppermute | solution.py:23
  17.3 2.0 %collective-permute-start.2 = (bf16[3,32,1536]{2,1,0:T(8,128)(2,1)S(1)}, bf16[3,32,1536]{2,1,0:T(8,128)(2,1)S(1)}, u32[]{:S(2)}, u32[]{:S(2)}) collective-permute-start(bf16[3,32,1536]{2,1,0:T(8,128)(2,1)S(1)} %pad_maximum_fusion.7), channel_id=1, source_target_pairs={{0,4},{4,0},{8,12},{12,8},{16,20},{20,16},{24,28},{28,24},{1,5},{5... | collective-permute-start | bytes 884744 | tf_op jit(solution)/shard_map/ppermute | solution.py:23
  19.2 1.2 %collective-permute-done.4 = bf16[3,16,1536]{2,1,0:T(8,128)(2,1)S(1)} collective-permute-done((bf16[3,16,1536]{2,1,0:T(8,128)(2,1)S(1)}, bf16[3,16,1536]{2,1,0:T(8,128)(2,1)S(1)}, u32[]{:S(2)}, u32[]{:S(2)}) %collective-permute-start.4) | collective-permute-done | bytes 147488 | tf_op jit(solution)/shard_map/ppermute | solution.py:23
  20.5 0.3 collective-permute-start.5
  20.8 6.5 %shard_map.84.w_ref = bf16[3072,3072]{1,0:T(8,128)(2,1)S(1)} custom-call(bf16[3072,3072]{1,0:T(8,128)(2,1)} %refs_0_.1, bf16[3,32,1536]{2,1,0:T(8,128)(2,1)S(1)} %pad_maximum_fusion.8.refs_1_), custom_call_target="tpu_custom_call" | custom-call | flops 1207959552 | bytes 18874368 | tf_op jit(solution)/shard_map/pallas_call | solution.py:47
  27.5 3.0 %shard_map.85 = (f32[64,3072]{1,0:T(8,128)S(1)}, f32[64,3072]{1,0:T(8,128)S(1)}, bf16[3072,3072]{1,0:T(8,128)(2,1)S(1)}) custom-call(s32[1]{0:T(128)} %bitcast.core_ref.refs_0_, bf16[192,1536]{1,0:T(8,128)(2,1)S(1)} %bitcast.14, bf16[192,1536]{1,0:T(8,128)(2,1)S(1)} %bitcast.16, bf16[3072,3072]{1,0:T(8,128)(2,1)S(1)} %shard_map.84.w_ref), custom_call_target="tpu_custom_call", output_to_operand_aliasing={{2}: (3, {})} | custom-call | flops 1207959552 | bytes 18874368 | tf_op jit(solution)/shard_map/pallas_call | solution.py:47
  30.7 2.2 %collective-permute-done.6 = f32[64,3072]{1,0:T(8,128)S(1)} collective-permute-done((f32[64,3072]{1,0:T(8,128)S(1)}, f32[64,3072]{1,0:T(8,128)S(1)}, u32[]{:S(2)}, u32[]{:S(2)}) %collective-permute-start.6) | collective-permute-done | bytes 786464 | tf_op jit(solution)/shard_map/ppermute | solution.py:23
  32.9 0.1 fusion.9
  33.0 1.6 %collective-permute-start.7 = (bf16[64,3072]{1,0:T(8,128)(2,1)S(1)}, bf16[64,3072]{1,0:T(8,128)(2,1)S(1)}, u32[]{:S(2)}, u32[]{:S(2)}) collective-permute-start(bf16[64,3072]{1,0:T(8,128)(2,1)S(1)} %get-tuple-element.34.refs_4_), channel_id=1, source_target_pairs={{0,2},{1,3},{2,0},{3,1},{4,6},{5,7},{6,4},{7,5},{8,10},{9,11},{10,... | collective-permute-start | bytes 1179656 | tf_op jit(solution)/shard_map/ppermute | solution.py:23
  34.6 8.4 %shard_map.86 = (f32[32,3072]{1,0:T(8,128)S(1)}, f32[32,3072]{1,0:T(8,128)S(1)}, bf16[3072,3072]{1,0:T(8,128)(2,1)S(1)}) custom-call(s32[1]{0:T(128)} %bitcast.core_ref.refs_0_, bf16[192,1536]{1,0:T(8,128)(2,1)S(1)} %bitcast.15, bf16[192,1536]{1,0:T(8,128)(2,1)S(1)} %bitcast.17, bf16[3072,3072]{1,0:T(8,128)(2,1)} %refs_3_.1, ...), custom_call_target="tpu_custom_call" | custom-call | flops 1207959552 | bytes 18874368 | tf_op jit(solution)/shard_map/pallas_call | solution.py:47
  43.1 1.1 %collective-permute-done.7 = bf16[64,3072]{1,0:T(8,128)(2,1)S(1)} collective-permute-done((bf16[64,3072]{1,0:T(8,128)(2,1)S(1)}, bf16[64,3072]{1,0:T(8,128)(2,1)S(1)}, u32[]{:S(2)}, u32[]{:S(2)}) %collective-permute-start.7) | collective-permute-done | bytes 393248 | tf_op jit(solution)/shard_map/ppermute | solution.py:23
  44.3 0.2 fusion.3
  44.5 0.3 collective-permute-done.9
  44.8 1.3 %collective-permute-start.11 = (bf16[32,3072]{1,0:T(8,128)(2,1)S(1)}, bf16[32,3072]{1,0:T(8,128)(2,1)S(1)}, u32[]{:S(2)}, u32[]{:S(2)}) collective-permute-start(bf16[32,3072]{1,0:T(8,128)(2,1)S(1)} %get-tuple-element.32.refs_4_), channel_id=1, source_target_pairs={{0,2},{1,3},{2,0},{3,1},{4,6},{5,7},{6,4},{7,5},{8,10},{9,11},{10,... | collective-permute-start | bytes 589832 | tf_op jit(solution)/shard_map/ppermute | solution.py:23
  46.3 5.6 %collective-permute-done.11 = bf16[32,3072]{1,0:T(8,128)(2,1)S(1)} collective-permute-done((bf16[32,3072]{1,0:T(8,128)(2,1)S(1)}, bf16[32,3072]{1,0:T(8,128)(2,1)S(1)}, u32[]{:S(2)}, u32[]{:S(2)}) %collective-permute-start.11) | collective-permute-done | bytes 196640 | tf_op jit(solution)/shard_map/ppermute | solution.py:23
  52.1 3.7 %shard_map.87 = (f32[32,3072]{1,0:T(8,128)S(1)}, bf16[32,3072]{1,0:T(8,128)(2,1)S(1)}) custom-call(s32[1]{0:T(128)} %bitcast.core_ref.refs_0_, bf16[32,3072]{1,0:T(8,128)(2,1)S(1)} %get-tuple-element.45.refs_1_, bf16[32,3072]{1,0:T(8,128)(2,1)S(1)} %get-tuple-element.46.refs_2_, bf16[3072,3072]{1,0:T(8,128)(2,1)S(1)} %get-tuple-element.21.refs_3_, ...), custom_call_target="tpu_custom_call" | custom-call | flops 1207959552 | bytes 18874368 | tf_op jit(solution)/shard_map/pallas_call | solution.py:47
  55.8 1.6 %collective-permute-start.10 = (bf16[32,3072]{1,0:T(8,128)(2,1)S(1)}, bf16[32,3072]{1,0:T(8,128)(2,1)S(1)}, u32[]{:S(2)}, u32[]{:S(2)}) collective-permute-start(bf16[32,3072]{1,0:T(8,128)(2,1)S(1)} %get-tuple-element.25.refs_4_), channel_id=1, source_target_pairs={{0,4},{4,0},{8,12},{12,8},{16,20},{20,16},{24,28},{28,24},{1,5},{5... | collective-permute-start | bytes 589832 | tf_op jit(solution)/shard_map/ppermute | solution.py:23
  57.4 6.3 %shard_map.88 = (f32[32,3072]{1,0:T(8,128)S(1)}, bf16[32,3072]{1,0:T(8,128)(2,1)S(1)}) custom-call(s32[1]{0:T(128)} %bitcast.core_ref.refs_0_, bf16[32,3072]{1,0:T(8,128)(2,1)S(1)} %multiply_convert_fusion.refs_1_, bf16[32,3072]{1,0:T(8,128)(2,1)S(1)} %collective-permute-done.12.refs_2_, bf16[3072,3072]{1,0:T(8,128)(2,1)S(1)} %get-tuple-element.27.refs_3_, ...), custom_call_target="tpu_custom_call" | custom-call | flops 1207959552 | bytes 18874368 | tf_op jit(solution)/shard_map/pallas_call | solution.py:47
  63.7 0.6 collective-permute-start.13
  64.4 6.4 %collective-permute-done.13 = bf16[32,3072]{1,0:T(8,128)(2,1)S(1)} collective-permute-done((bf16[32,3072]{1,0:T(8,128)(2,1)S(1)}, bf16[32,3072]{1,0:T(8,128)(2,1)S(1)}, u32[]{:S(2)}, u32[]{:S(2)}) %collective-permute-start.13) | collective-permute-done | bytes 196640 | tf_op jit(solution)/shard_map/ppermute | solution.py:23
  70.8 1.8 %collective-permute-start.14 = (bf16[16,6144]{1,0:T(8,128)(2,1)S(1)}, bf16[16,6144]{1,0:T(8,128)(2,1)S(1)}, u32[]{:S(2)}, u32[]{:S(2)}) collective-permute-start(bf16[16,6144]{1,0:T(8,128)(2,1)S(1)} %fusion.6.refs_5_), channel_id=1, source_target_pairs={{0,8},{4,12},{8,0},{12,4},{16,24},{20,28},{24,16},{28,20},{1,9},{5... | collective-permute-start | bytes 589832 | tf_op jit(solution)/shard_map/ppermute | solution.py:23
  72.7 5.7 %shard_map.89.refs_4_ = bf16[3072,3072]{1,0:T(8,128)(2,1)} custom-call(bf16[64,3072]{1,0:T(8,128)(2,1)S(1)} %pad_maximum_fusion.5.refs_0_, bf16[64,3072]{1,0:T(8,128)(2,1)S(1)} %pad_maximum_fusion.6.refs_1_, bf16[32,3072]{1,0:T(8,128)(2,1)S(1)} %get-tuple-element.29.refs_2_), custom_call_target="tpu_custom_call" | custom-call | flops 805306368 | bytes 12582912 | tf_op jit(solution)/shard_map/pallas_call | solution.py:47
  78.6 2.2 %collective-permute-start.15 = (bf16[8,6144]{1,0:T(8,128)(2,1)S(1)}, bf16[8,6144]{1,0:T(8,128)(2,1)S(1)}, u32[]{:S(2)}, u32[]{:S(2)}) collective-permute-start(bf16[8,6144]{1,0:T(8,128)(2,1)S(1)} %slice.171.refs_3_), channel_id=1, source_target_pairs={{0,16},{4,20},{8,24},{12,28},{16,0},{20,4},{24,8},{28,12},{1,17},{... | collective-permute-start | bytes 294920 | tf_op jit(solution)/shard_map/ppermute | solution.py:23
  80.8 5.7 %shard_map.90 = (bf16[3072,3072]{1,0:T(8,128)(2,1)}, bf16[3072,3072]{1,0:T(8,128)(2,1)}) custom-call(bf16[64,3072]{1,0:T(8,128)(2,1)S(1)} %pad_maximum_fusion.5.refs_0_, bf16[64,3072]{1,0:T(8,128)(2,1)S(1)} %pad_maximum_fusion.6.refs_1_, bf16[64,3072]{1,0:T(8,128)(2,1)S(1)} %get-tuple-element.54.refs_2_.refs_0_, ...), custom_call_target="tpu_custom_call", output_to_operand_aliasing={{0}: (4, {})} | custom-call | flops 805306368 | bytes 12582912 | tf_op jit(solution)/shard_map/pallas_call | solution.py:47
  86.5 5.7 %shard_map.91 = bf16[3072,3072]{1,0:T(8,128)(2,1)} custom-call(bf16[64,3072]{1,0:T(8,128)(2,1)S(1)} %get-tuple-element.54.refs_2_.refs_0_, bf16[64,3072]{1,0:T(8,128)(2,1)S(1)} %get-tuple-element.55.refs_3_.refs_1_, bf16[3072,3072]{1,0:T(8,128)(2,1)} %get-tuple-element.30.refs_2_, bf16[8,6144]{1,0:T(8,128)(2,1)S(1)} %slice.171.refs_3_), custom_call_target="tpu_custom_call", output_to_operand_aliasing={{}: (2, {})} | custom-call | flops 805306368 | bytes 12582912 | tf_op jit(solution)/shard_map/pallas_call | solution.py:47
  92.3 0.6 fusion.11
  (42 shorter events, 1.1 us)
Async XLA Ops:
  1.5 8.0 %collective-permute-start = (bf16[3,8,1536]{2,1,0:T(8,128)(2,1)S(1)}, bf16[3,8,1536]{2,1,0:T(8,128)(2,1)S(1)}, u32[]{:S(2)}, u32[]{:S(2)}) collective-permute-start(bf16[3,8,1536]{2,1,0:T(8,128)(2,1)S(1)} %get-tuple-element.51), channel_id=1, source_target_pairs={{0,16},{4,20},{8,24},{12,28},{16,0},{20,4},{24,8},{28,12},{1,17},{... | collective-permute-start | bytes 221192 | tf_op jit(solution)/shard_map/ppermute | solution.py:23
  5.7 4.7 %collective-permute-start.3 = (bf16[3,8,1536]{2,1,0:T(8,128)(2,1)S(1)}, bf16[3,8,1536]{2,1,0:T(8,128)(2,1)S(1)}, u32[]{:S(2)}, u32[]{:S(2)}) collective-permute-start(bf16[3,8,1536]{2,1,0:T(8,128)(2,1)S(1)} %get-tuple-element.49), channel_id=1, source_target_pairs={{0,4},{4,0},{8,12},{12,8},{16,20},{20,16},{24,28},{28,24},{1,5},{5... | collective-permute-start | bytes 221192 | tf_op jit(solution)/shard_map/ppermute | solution.py:23
  9.6 7.7 %collective-permute-start.1 = (bf16[3,16,1536]{2,1,0:T(8,128)(2,1)S(1)}, bf16[3,16,1536]{2,1,0:T(8,128)(2,1)S(1)}, u32[]{:S(2)}, u32[]{:S(2)}) collective-permute-start(bf16[3,16,1536]{2,1,0:T(8,128)(2,1)S(1)} %pad_maximum_fusion.10), channel_id=1, source_target_pairs={{0,8},{4,12},{8,0},{12,4},{16,24},{20,28},{24,16},{28,20},{1,9},{5... | collective-permute-start | bytes 442376 | tf_op jit(solution)/shard_map/ppermute | solution.py:23
  10.3 10.2 %collective-permute-start.4 = (bf16[3,16,1536]{2,1,0:T(8,128)(2,1)S(1)}, bf16[3,16,1536]{2,1,0:T(8,128)(2,1)S(1)}, u32[]{:S(2)}, u32[]{:S(2)}) collective-permute-start(bf16[3,16,1536]{2,1,0:T(8,128)(2,1)S(1)} %pad_maximum_fusion.11), channel_id=1, source_target_pairs={{0,16},{4,20},{8,24},{12,28},{16,0},{20,4},{24,8},{28,12},{1,17},{... | collective-permute-start | bytes 442376 | tf_op jit(solution)/shard_map/ppermute | solution.py:23
  17.3 10.1 %collective-permute-start.2 = (bf16[3,32,1536]{2,1,0:T(8,128)(2,1)S(1)}, bf16[3,32,1536]{2,1,0:T(8,128)(2,1)S(1)}, u32[]{:S(2)}, u32[]{:S(2)}) collective-permute-start(bf16[3,32,1536]{2,1,0:T(8,128)(2,1)S(1)} %pad_maximum_fusion.7), channel_id=1, source_target_pairs={{0,4},{4,0},{8,12},{12,8},{16,20},{20,16},{24,28},{28,24},{1,5},{5... | collective-permute-start | bytes 884744 | tf_op jit(solution)/shard_map/ppermute | solution.py:23
  20.5 6.9 %collective-permute-start.5 = (bf16[3,32,1536]{2,1,0:T(8,128)(2,1)S(1)}, bf16[3,32,1536]{2,1,0:T(8,128)(2,1)S(1)}, u32[]{:S(2)}, u32[]{:S(2)}) collective-permute-start(bf16[3,32,1536]{2,1,0:T(8,128)(2,1)S(1)} %pad_maximum_fusion.8.refs_1_), channel_id=1, source_target_pairs={{0,8},{4,12},{8,0},{12,4},{16,24},{20,28},{24,16},{28,20},{1,9},{5... | collective-permute-start | bytes 884744 | tf_op jit(solution)/shard_map/ppermute | solution.py:23
  30.5 2.4 %collective-permute-start.6 = (f32[64,3072]{1,0:T(8,128)S(1)}, f32[64,3072]{1,0:T(8,128)S(1)}, u32[]{:S(2)}, u32[]{:S(2)}) collective-permute-start(f32[64,3072]{1,0:T(8,128)S(1)} %get-tuple-element.19), channel_id=1, source_target_pairs={{0,1},{1,0},{2,3},{3,2},{4,5},{5,4},{6,7},{7,6},{8,9},{9,8},{10,11... | collective-permute-start | bytes 2359304 | tf_op jit(solution)/shard_map/ppermute | solution.py:23
  33.0 11.2 %collective-permute-start.7 = (bf16[64,3072]{1,0:T(8,128)(2,1)S(1)}, bf16[64,3072]{1,0:T(8,128)(2,1)S(1)}, u32[]{:S(2)}, u32[]{:S(2)}) collective-permute-start(bf16[64,3072]{1,0:T(8,128)(2,1)S(1)} %get-tuple-element.34.refs_4_), channel_id=1, source_target_pairs={{0,2},{1,3},{2,0},{3,1},{4,6},{5,7},{6,4},{7,5},{8,10},{9,11},{10,... | collective-permute-start | bytes 1179656 | tf_op jit(solution)/shard_map/ppermute | solution.py:23
  43.0 1.8 %collective-permute-start.9 = (f32[32,3072]{1,0:T(8,128)S(1)}, f32[32,3072]{1,0:T(8,128)S(1)}, u32[]{:S(2)}, u32[]{:S(2)}) collective-permute-start(f32[32,3072]{1,0:T(8,128)S(1)} %get-tuple-element.23), channel_id=1, source_target_pairs={{0,1},{1,0},{2,3},{3,2},{4,5},{5,4},{6,7},{7,6},{8,9},{9,8},{10,11... | collective-permute-start | bytes 1179656 | tf_op jit(solution)/shard_map/ppermute | solution.py:23
  44.8 7.0 %collective-permute-start.11 = (bf16[32,3072]{1,0:T(8,128)(2,1)S(1)}, bf16[32,3072]{1,0:T(8,128)(2,1)S(1)}, u32[]{:S(2)}, u32[]{:S(2)}) collective-permute-start(bf16[32,3072]{1,0:T(8,128)(2,1)S(1)} %get-tuple-element.32.refs_4_), channel_id=1, source_target_pairs={{0,2},{1,3},{2,0},{3,1},{4,6},{5,7},{6,4},{7,5},{8,10},{9,11},{10,... | collective-permute-start | bytes 589832 | tf_op jit(solution)/shard_map/ppermute | solution.py:23
  46.2 5.8 %collective-permute-start.8 = (bf16[64,3072]{1,0:T(8,128)(2,1)S(1)}, bf16[64,3072]{1,0:T(8,128)(2,1)S(1)}, u32[]{:S(2)}, u32[]{:S(2)}) collective-permute-start(bf16[64,3072]{1,0:T(8,128)(2,1)S(1)} %pad_maximum_fusion.2), channel_id=1, source_target_pairs={{0,1},{1,0},{2,3},{3,2},{4,5},{5,4},{6,7},{7,6},{8,9},{9,8},{10,11... | collective-permute-start | bytes 1179656 | tf_op jit(solution)/shard_map/ppermute | solution.py:23
  51.9 5.5 %collective-permute-start.12 = (bf16[32,3072]{1,0:T(8,128)(2,1)S(1)}, bf16[32,3072]{1,0:T(8,128)(2,1)S(1)}, u32[]{:S(2)}, u32[]{:S(2)}) collective-permute-start(bf16[32,3072]{1,0:T(8,128)(2,1)S(1)} %multiply_convert_fusion.refs_1_), channel_id=1, source_target_pairs={{0,1},{1,0},{2,3},{3,2},{4,5},{5,4},{6,7},{7,6},{8,9},{9,8},{10,11... | collective-permute-start | bytes 589832 | tf_op jit(solution)/shard_map/ppermute | solution.py:23
  55.8 8.5 %collective-permute-start.10 = (bf16[32,3072]{1,0:T(8,128)(2,1)S(1)}, bf16[32,3072]{1,0:T(8,128)(2,1)S(1)}, u32[]{:S(2)}, u32[]{:S(2)}) collective-permute-start(bf16[32,3072]{1,0:T(8,128)(2,1)S(1)} %get-tuple-element.25.refs_4_), channel_id=1, source_target_pairs={{0,4},{4,0},{8,12},{12,8},{16,20},{20,16},{24,28},{28,24},{1,5},{5... | collective-permute-start | bytes 589832 | tf_op jit(solution)/shard_map/ppermute | solution.py:23
  63.7 7.1 %collective-permute-start.13 = (bf16[32,3072]{1,0:T(8,128)(2,1)S(1)}, bf16[32,3072]{1,0:T(8,128)(2,1)S(1)}, u32[]{:S(2)}, u32[]{:S(2)}) collective-permute-start(bf16[32,3072]{1,0:T(8,128)(2,1)S(1)} %get-tuple-element.29.refs_2_), channel_id=1, source_target_pairs={{0,4},{4,0},{8,12},{12,8},{16,20},{20,16},{24,28},{28,24},{1,5},{5... | collective-permute-start | bytes 589832 | tf_op jit(solution)/shard_map/ppermute | solution.py:23
  70.8 7.7 %collective-permute-start.14 = (bf16[16,6144]{1,0:T(8,128)(2,1)S(1)}, bf16[16,6144]{1,0:T(8,128)(2,1)S(1)}, u32[]{:S(2)}, u32[]{:S(2)}) collective-permute-start(bf16[16,6144]{1,0:T(8,128)(2,1)S(1)} %fusion.6.refs_5_), channel_id=1, source_target_pairs={{0,8},{4,12},{8,0},{12,4},{16,24},{20,28},{24,16},{28,20},{1,9},{5... | collective-permute-start | bytes 589832 | tf_op jit(solution)/shard_map/ppermute | solution.py:23
  78.6 13.7 %collective-permute-start.15 = (bf16[8,6144]{1,0:T(8,128)(2,1)S(1)}, bf16[8,6144]{1,0:T(8,128)(2,1)S(1)}, u32[]{:S(2)}, u32[]{:S(2)}) collective-permute-start(bf16[8,6144]{1,0:T(8,128)(2,1)S(1)} %slice.171.refs_3_), channel_id=1, source_target_pairs={{0,16},{4,20},{8,24},{12,28},{16,0},{20,4},{24,8},{28,12},{1,17},{... | collective-permute-start | bytes 294920 | tf_op jit(solution)/shard_map/ppermute | solution.py:23

commit v3 on v2

--- a/solution.py
+++ b/solution.py
@@ -9,7 +9,7 @@
 BF16, F32 = jnp.bfloat16, jnp.float32
 MIB = 1 << 20
 FLOPS = 128
-NN, NT, TN = ((1,), (0,)), ((1,), (1,)), ((0,), (0,))
+NN, NT = ((1,), (0,)), ((1,), (1,))
 
 
 def gelu_parts(pre):
@@ -61,33 +61,32 @@
 HBM = pl.BlockSpec(memory_space=pltpu.HBM)
 
 
-def core():
-    return lax.rem(lax.axis_index("col"), 2)
-
-
-def load(w, after, parts=8):
-    rows = w.shape[0] // parts
-
-    def kernel(w_ref, o_ref, sems):
-        copies = [
-            pltpu.make_async_copy(w_ref.at[pl.ds(i * rows, rows)], o_ref.at[pl.ds(i * rows, rows)], sems.at[i])
-            for i in range(parts)
-        ]
-        for copy in copies:
-            copy.start()
+def load(w, held, first, rows, after, parts=4):
+    step = rows // parts
+    old = [] if held is None else [pltpu.with_memory_space_constraint(held, pltpu.VMEM)]
+
+    def kernel(w_ref, *refs):
+        o_ref, sems = refs[-2:]
+        copies = []
+        for i in range(parts):
+            part = pl.ds(first + i * step, step)
+            copies.append(pltpu.make_async_copy(w_ref.at[part], o_ref.at[part], sems.at[i]))
+            copies[-1].start()
         for copy in copies:
             copy.wait()
 
     return call(
         kernel,
-        [HBM],
+        [HBM] + [VMEM] * len(old),
         VMEM,
         pltpu.VMEM(w.shape, w.dtype),
         [pltpu.SemaphoreType.DMA((parts,))],
-        w.size,
-        2 * w.size,
+        rows * w.shape[1],
+        2 * rows * w.shape[1],
         pltpu.with_memory_space_constraint(w, pltpu.HBM),
+        *old,
         grant=2,
+        aliases={1: 0} if old else {},
         after=after,
     )
 
@@ -118,13 +117,12 @@
         body(part(j))
 
 
-def into(x, y, w, rows, dims, after=None):
+def into(me, x, y, w, rows, dims, here, sends, after=None):
     free = 1 - dims[1][0]
     k, n = w.shape[dims[1][0]], w.shape[free]
     h = x.shape[1]
     first, count, groups = rows
     tall = count // groups // 2
-    here = after is None
     b = block_of(n, 1024 if here else 512)
 
     def kernel(core_ref, x_ref, y_ref, w_ref, mine_ref, send_ref, held, *sems):
@@ -137,24 +135,26 @@
                 left, right = w_from[:h, part], w_from[h:, part]
             else:
                 left, right = w_from[part, :h], w_from[part, h:]
-            acc = dot(x_ref[one, :], left, dims) + dot(y_ref[one, :], right, dims)
+            if free == 1:
+                acc = dot(x_ref[one, :], left, NN) + dot(y_ref[one, :], right, NN)
+            else:
+                acc = (dot(left, x_ref[one, :], NT) + dot(right, y_ref[one, :], NT)).T
             for g in range(groups):
                 at = 2 * g * tall
                 lo, hi = acc[at : at + tall], acc[at + tall : at + 2 * tall]
                 put = pl.ds(g * tall, tall)
                 mine_ref[put, part] = jnp.where(low, lo, hi)
-                send_ref[put, part] = jnp.where(low, hi, lo)
+                send_ref[put, part] = jnp.where(low, hi, lo).astype(sends)
 
         stream(w_ref, held, None if here else sems[0], b, free, body)
 
-    shape = jax.ShapeDtypeStruct((count // 2, n), F32)
-    me = jnp.full((1,), core(), jnp.int32)
+    half = count // 2, n
     space = pltpu.VMEM if here else pltpu.HBM
     return call(
         kernel,
         [SMEM, VMEM, VMEM, VMEM if here else HBM],
         [VMEM, VMEM, VMEM],
-        [shape, shape, pltpu.VMEM(w.shape, w.dtype)],
+        [jax.ShapeDtypeStruct(half, F32), jax.ShapeDtypeStruct(half, sends), pltpu.VMEM(w.shape, w.dtype)],
         [] if here else [pltpu.SemaphoreType.DMA((n // b,))],
         k * n,
         2 * k * n,
@@ -167,34 +167,39 @@
     )
 
 
-def outof(own, other, w, dims, here, after):
+def outof(me, own, other, w, dims, here, after):
     free = 1 - dims[1][0]
     k, n = w.shape[dims[1][0]], w.shape[free]
     half = own.shape[0]
+    tall = max(2 * half, 128 if free == 1 else 0)
     b = block_of(n, 1024 if here else 512)
 
     def kernel(core_ref, own_ref, other_ref, w_ref, keep_ref, send_ref, x_ref, *scratch):
         low = core_ref[0] == 0
         one, two = own_ref[...], other_ref[...]
         x_ref[:half, :] = jnp.where(low, one, two)
-        x_ref[half:, :] = jnp.where(low, two, one)
+        x_ref[half : 2 * half, :] = jnp.where(low, two, one)
+        if tall > 2 * half:
+            x_ref[2 * half :, :] = jnp.zeros((tall - 2 * half, k), BF16)
         held, sems = scratch or (w_ref, None)
 
         def body(part):
-            acc = dot(x_ref[...], held[:, part] if free == 1 else held[part, :], dims)
+            if free == 1:
+                acc = dot(x_ref[...], held[:, part], NN)
+            else:
+                acc = dot(held[part, :], x_ref[...], NT).T
             keep_ref[:, part] = acc[:half]
-            send_ref[:, part] = acc[half:].astype(BF16)
+            send_ref[:, part] = acc[half : 2 * half].astype(BF16)
 
         stream(w_ref, held, sems, b, free, body)
 
-    me = jnp.full((1,), core(), jnp.int32)
     scratch = [] if here else [pltpu.VMEM(w.shape, w.dtype), pltpu.SemaphoreType.DMA((n // b,))]
     return call(
         kernel,
         [SMEM, VMEM, VMEM, VMEM if here else HBM],
         [VMEM, VMEM],
         [jax.ShapeDtypeStruct((half, n), F32), jax.ShapeDtypeStruct((half, n), BF16)],
-        [pltpu.VMEM((2 * half, k), BF16), *scratch],
+        [pltpu.VMEM((tall, k), BF16), *scratch],
         k * n,
         2 * k * n,
         me,
@@ -209,25 +214,34 @@
 def outer(jobs, after):
     blocks, olds = [], []
     for i, (x, _, old, first, rows) in enumerate(jobs):
-        b = block_of(rows, 512)
+        b = block_of(rows, 1024)
         blocks += [(i, first + j, b) for j in range(0, rows, b)]
         if old is not None:
             olds.append((i, pltpu.with_memory_space_constraint(old, pltpu.HBM)))
     tall = max(b for _, _, b in blocks)
-    width = jobs[0][1].shape[1]
+    depth, width = jobs[0][1].shape
     count = len(jobs)
+    sizes = [width]
+    while len(sizes) < 4 and sizes[-1] % 256 == 0:
+        sizes[-1:] = [sizes[-1] // 2] * 2
+    cuts = [sizes[::-1]] + [sizes[:1] + [width - sizes[0]]] * (len(blocks) - 2) + [sizes]
+    columns = [[(sum(cut[:i]), n) for i, n in enumerate(cut) if n] for cut in cuts[-len(blocks) :]]
 
     def kernel(*refs):
         sides = refs[: 2 * count]
         outs = refs[2 * count + len(olds) : 3 * count + len(olds)]
-        held, sems = refs[3 * count + len(olds) :]
+        held, turned, sems = refs[3 * count + len(olds) :]
         copies = []
         for at, (i, row, b) in enumerate(blocks):
             part = pl.ds(row, b)
-            space = held.at[at, pl.ds(0, b)]
-            space[...] = dot(sides[2 * i][:, part], sides[2 * i + 1][...], TN).astype(BF16)
-            copies.append(pltpu.make_async_copy(space, outs[i].at[part], sems.at[at]))
-            copies[-1].start()
+            turned[at, :b, :] = sides[2 * i][:, part].T
+            for c, n in columns[at]:
+                here = pl.ds(c, n)
+                held[at, :b, here] = dot(turned[at, :b, :], sides[2 * i + 1][:, here], NN).astype(BF16)
+                copies.append(
+                    pltpu.make_async_copy(held.at[at, pl.ds(0, b), here], outs[i].at[part, here], sems.at[len(copies)])
+                )
+                copies[-1].start()
         for copy in copies:
             copy.wait()
 
@@ -237,7 +251,11 @@
         [VMEM] * (2 * count) + [HBM] * len(olds),
         [HBM] * count,
         [pltpu.HBM((x.shape[1], width), BF16) for x, *_ in jobs],
-        [pltpu.VMEM((len(blocks), tall, width), BF16), pltpu.SemaphoreType.DMA((len(blocks),))],
+        [
+            pltpu.VMEM((len(blocks), tall, width), BF16),
+            pltpu.VMEM((len(blocks), tall, depth), BF16),
+            pltpu.SemaphoreType.DMA((sum(len(c) for c in columns),)),
+        ],
         moved,
         2 * moved,
         *[side for x, y, *_ in jobs for side in (x, y)],
@@ -252,10 +270,10 @@
     all_bits = bits(lax.axis_size("row"))
     one = all_bits[::-1]
     two = all_bits[:1] + all_bits[:0:-1]
-    order_one, order_two = [0], [0]
+    order_one, order_two, ready = [0], [0], []
     tall = left.shape[1]
     for a, b in zip(one, two):
-        last = right
+        ready.append(right)
         from_left, from_right = swap(left, "row", a), swap(right, "row", b)
         left = jnp.concatenate([left, from_left], axis=1)
         right = jnp.concatenate([right, from_right], axis=1)
@@ -263,11 +281,11 @@
         order_two += [j ^ b for j in order_two]
     at = [order_two.index(j) * tall for j in order_one]
     right = jnp.concatenate([right[:, i : i + tall] for i in at], axis=1)
-    return left, right, last
+    return left, right, ready
 
 
 def pair_sum(mine, send):
-    return mine + swap(send, "col", 1)
+    return mine + swap(send, "col", 1).astype(F32)
 
 
 def col_send(x):
@@ -281,40 +299,47 @@
     return x
 
 
-def in_order(own, other):
-    low = core() == 0
+def in_order(low, own, other):
     return jnp.concatenate([jnp.where(low, own, other), jnp.where(low, other, own)], axis=0)
 
 
 def local(tokens, past_tokens, out_grad, w_in, w_out):
-    x = lax.optimization_barrier(jnp.stack([tokens, past_tokens, out_grad]))
+    me = lax.rem(lax.axis_index("col"), 2)
+    x = jnp.stack([tokens, past_tokens, out_grad])
+    x, me, low = lax.optimization_barrier((x, me.reshape(1), me == 0))
     width = x.shape[2]
     h = width // 2
-    left, right, last = gather(x[:, :, :h], x[:, :, h:])
+    left, right, ready = gather(x[:, :, :h], x[:, :, h:])
     n = left.shape[1]
     half = n // 2
     left, right = left.reshape(3 * n, h), right.reshape(3 * n, h)
-    mine, send, w_in_here = into(left, right, load(w_in, last), (0, 2 * n, 2), NN)
+    w_in_here = load(w_in, None, 0, w_in.shape[0], ready[-1], 8)
+    part = w_out.shape[0] // 2
+    w_out_here = load(w_out, None, 0, part, ready[-3])
+    w_out_here = load(w_out, w_out_here, part, part, ready[-2])
+    mine, send, w_in_here = into(me, left, right, w_in_here, (0, 2 * n, 2), NN, True, BF16)
     pre = pair_sum(mine, send)
-    pre_sent = col_send(pre)
-    mine, send, w_out_here = into(left, right, w_out, (2 * n, n, 1), NT, pre_sent)
+    sent = lax.optimization_barrier((pre[:half].astype(BF16), pre[half:].astype(BF16)))
+    mine, send, w_out_here = into(me, left, right, w_out_here, (2 * n, n, 1), NT, True, F32, sent[0])
     back = pair_sum(mine, send)
     back_sent = col_send(back)
-    pre = col_sum(pre, pre_sent)
-    hidden = gelu_parts(pre[:half])[0]
-    act, slope = gelu_parts(pre[half:])
-    own, slope = lax.optimization_barrier((jnp.concatenate([hidden, act], axis=0).astype(BF16), slope))
+    past = col_sum(pre[half:], sent[1])
+    act, slope = gelu_parts(past)
+    act, slope = lax.optimization_barrier((act.astype(BF16), slope))
+    now = col_sum(pre[:half], sent[0])
+    hidden = gelu_parts(now)[0].astype(BF16)
+    own, slope = lax.optimization_barrier((jnp.concatenate([hidden, act], axis=0), slope))
     other = swap(own, "col", 1)
-    layer = outof(own[:half], other[:half], w_out_here, NN, True, back_sent)
+    layer = outof(me, own[:half], other[:half], w_out_here, NN, True, back_sent)
     back = col_sum(back, back_sent)
     own_grad = (back * slope).astype(BF16)
     other_grad = swap(own_grad, "col", 1)
-    inp = outof(own_grad, other_grad, w_in_here, NT, True, layer[1])
+    inp = outof(me, own_grad, other_grad, w_in_here, NT, True, layer[1])
     past_all = jnp.concatenate([left[n : 2 * n], right[n : 2 * n]], axis=1)
     grad_all = jnp.concatenate([left[2 * n :], right[2 * n :]], axis=1)
     row_bits = bits(lax.axis_size("row"))
     sums = [keep + swap(send, "row", row_bits[0]).astype(F32) for (keep, send) in (layer, inp)]
-    act_all, hidden_grad = in_order(own[half:], other[half:]), in_order(own_grad, other_grad)
+    act_all, hidden_grad = in_order(low, own[half:], other[half:]), in_order(low, own_grad, other_grad)
     units = act_all.shape[1], past_all.shape[1]
     share = units[0] * 2 // 3 // 128 * 128, units[1] // 3 // 128 * 128
     (grad_w_out,) = outer([(act_all, grad_all, None, 0, share[0])], inp[1])

time: 93.1 us -> 95.8 us (1.029)
  Pallas kernels: 45.1 us -> 48.8 us
  starting transfers between devices: 21.5 us -> 17.9 us
  waiting for transfers between devices: 22.7 us -> 25.2 us
    pallas_call x8 -> x10, Pallas kernels: 45.1 us -> 48.8 us  [call(): pl.pallas_call(body, in_specs=in_specs, out_specs=out_specs, out_shape=ou...]
    ppermute x16 -> x17, starting transfers between devices: 21.5 us -> 17.9 us  [swap(): return lax.ppermute(x, axis, [(i, i ^ bit) for i in range(n)])]
    ppermute x16 -> x17, waiting for transfers between devices: 22.7 us -> 25.2 us  [swap(): return lax.ppermute(x, axis, [(i, i ^ bit) for i in range(n)])]
  transfers between devices with their start and end apart: 16 -> 17, of which waited for: 8 -> 8; matrix products, arithmetic and copies ran while one was open for 1% -> 1% of each run, Pallas kernels for 45% -> 48%
where the time goes in v3:
time: 95.8 us; the launch traced here: 95.6 us
  Pallas kernels  48.8 us (51%)
  waiting for transfers between devices  25.2 us (26%)
  starting transfers between devices  17.9 us (19%)
  other arithmetic  1.87 us (2%)
  between operations  0.99 us (1%)
    pallas_call x10, Pallas kernels, call(): pl.pallas_call(body, in_specs=in_specs, out_specs=out_specs, out_shape=ou...  48.8 us
    ppermute x17, waiting for transfers between devices, swap(): return lax.ppermute(x, axis, [(i, i ^ bit) for i in range(n)])  25.2 us
    ppermute x17, starting transfers between devices, swap(): return lax.ppermute(x, axis, [(i, i ^ bit) for i in range(n)])  17.9 us
  transfers between devices with their start and end apart: 17, of which 8 were waited for; matrix products, arithmetic and copies ran while one was open for 1% of the time, Pallas kernels for 48%

profile of v3, /device:TPU:0, one launch (start us, length us, event | category | flops | bytes accessed | tf_op | source)
XLA Modules:
  0.0 95.6 jit_solution(1189170571404334886)
XLA Ops:
  0.6 0.9 pad_maximum_fusion.9
  1.5 3.0 %collective-permute-start.3 = (bf16[3,8,1536]{2,1,0:T(8,128)(2,1)S(1)}, bf16[3,8,1536]{2,1,0:T(8,128)(2,1)S(1)}, u32[]{:S(2)}, u32[]{:S(2)}) collective-permute-start(bf16[3,8,1536]{2,1,0:T(8,128)(2,1)S(1)} %get-tuple-element.63.refs_1_), channel_id=1, source_target_pairs={{0,4},{4,0},{8,12},{12,8},{16,20},{20,16},{24,28},{28,24},{1,5},{5... | collective-permute-start | bytes 221192 | tf_op jit(solution)/shard_map/ppermute | solution.py:23
  4.6 2.6 %collective-permute-start = (bf16[3,8,1536]{2,1,0:T(8,128)(2,1)S(1)}, bf16[3,8,1536]{2,1,0:T(8,128)(2,1)S(1)}, u32[]{:S(2)}, u32[]{:S(2)}) collective-permute-start(bf16[3,8,1536]{2,1,0:T(8,128)(2,1)S(1)} %get-tuple-element.65), channel_id=1, source_target_pairs={{0,16},{4,20},{8,24},{12,28},{16,0},{20,4},{24,8},{28,12},{1,17},{... | collective-permute-start | bytes 221192 | tf_op jit(solution)/shard_map/ppermute | solution.py:23
  7.2 3.8 %shard_map.86.refs_1_ = bf16[3072,3072]{1,0:T(8,128)(2,1)S(1)} custom-call(bf16[3072,3072]{1,0:T(8,128)(2,1)} %refs_0_.5, bf16[3,8,1536]{2,1,0:T(8,128)(2,1)S(1)} %get-tuple-element.63.refs_1_), custom_call_target="tpu_custom_call" | custom-call | flops 603979776 | bytes 9437184 | tf_op jit(solution)/shard_map/pallas_call | solution.py:47
  11.0 0.4 collective-permute-start.4
  11.4 1.6 %collective-permute-start.1 = (bf16[3,16,1536]{2,1,0:T(8,128)(2,1)S(1)}, bf16[3,16,1536]{2,1,0:T(8,128)(2,1)S(1)}, u32[]{:S(2)}, u32[]{:S(2)}) collective-permute-start(bf16[3,16,1536]{2,1,0:T(8,128)(2,1)S(1)} %pad_maximum_fusion.10), channel_id=1, source_target_pairs={{0,8},{4,12},{8,0},{12,4},{16,24},{20,28},{24,16},{28,20},{1,9},{5... | collective-permute-start | bytes 442376 | tf_op jit(solution)/shard_map/ppermute | solution.py:23
  13.1 3.8 %shard_map.87.refs_3_ = bf16[3072,3072]{1,0:T(8,128)(2,1)S(1)} custom-call(bf16[3072,3072]{1,0:T(8,128)(2,1)} %refs_0_.5, bf16[3072,3072]{1,0:T(8,128)(2,1)S(1)} %shard_map.86.refs_1_, bf16[3,16,1536]{2,1,0:T(8,128)(2,1)S(1)} %pad_maximum_fusion.11.refs_2_), custom_call_target="tpu_custom_call", output_to_operand_aliasing={{}: (1, {})} | custom-call | flops 603979776 | bytes 9437184 | tf_op jit(solution)/shard_map/pallas_call | solution.py:47
  16.9 3.3 %collective-permute-done.4 = bf16[3,16,1536]{2,1,0:T(8,128)(2,1)S(1)} collective-permute-done((bf16[3,16,1536]{2,1,0:T(8,128)(2,1)S(1)}, bf16[3,16,1536]{2,1,0:T(8,128)(2,1)S(1)}, u32[]{:S(2)}, u32[]{:S(2)}) %collective-permute-start.4) | collective-permute-done | bytes 147488 | tf_op jit(solution)/shard_map/ppermute | solution.py:23
  20.3 6.5 %shard_map.84.w_ref = bf16[3072,3072]{1,0:T(8,128)(2,1)S(1)} custom-call(bf16[3072,3072]{1,0:T(8,128)(2,1)} %refs_0_.3, bf16[3,32,1536]{2,1,0:T(8,128)(2,1)S(1)} %pad_maximum_fusion.8.refs_1_), custom_call_target="tpu_custom_call" | custom-call | flops 1207959552 | bytes 18874368 | tf_op jit(solution)/shard_map/pallas_call | solution.py:47
  26.9 0.6 collective-permute-start.2
  27.5 0.2 collective-permute-done.5
  27.8 6.5 %collective-permute-done.2 = bf16[3,32,1536]{2,1,0:T(8,128)(2,1)S(1)} collective-permute-done((bf16[3,32,1536]{2,1,0:T(8,128)(2,1)S(1)}, bf16[3,32,1536]{2,1,0:T(8,128)(2,1)S(1)}, u32[]{:S(2)}, u32[]{:S(2)}) %collective-permute-start.2) | collective-permute-done | bytes 294944 | tf_op jit(solution)/shard_map/ppermute | solution.py:23
  34.4 3.1 %shard_map.85 = (f32[64,3072]{1,0:T(8,128)S(1)}, bf16[64,3072]{1,0:T(8,128)(2,1)S(1)}, bf16[3072,3072]{1,0:T(8,128)(2,1)S(1)}) custom-call(s32[1]{0:T(128)} %bitcast.3.core_ref.refs_0_, bf16[192,1536]{1,0:T(8,128)(2,1)S(1)} %bitcast.14, bf16[192,1536]{1,0:T(8,128)(2,1)S(1)} %bitcast.16, ...), custom_call_target="tpu_custom_call", output_to_operand_aliasing={{2}: (3, {})} | custom-call | flops 1207959552 | bytes 18874368 | tf_op jit(solution)/shard_map/pallas_call | solution.py:47
  37.6 1.7 %collective-permute-done.6 = bf16[64,3072]{1,0:T(8,128)(2,1)S(1)} collective-permute-done((bf16[64,3072]{1,0:T(8,128)(2,1)S(1)}, bf16[64,3072]{1,0:T(8,128)(2,1)S(1)}, u32[]{:S(2)}, u32[]{:S(2)}) %collective-permute-start.6) | collective-permute-done | bytes 393248 | tf_op jit(solution)/shard_map/ppermute | solution.py:23
  39.4 1.6 %collective-permute-start.7 = (bf16[32,3072]{1,0:T(8,128)(2,1)S(1)}, bf16[32,3072]{1,0:T(8,128)(2,1)S(1)}, u32[]{:S(2)}, u32[]{:S(2)}) collective-permute-start(bf16[32,3072]{1,0:T(8,128)(2,1)S(1)} %get-tuple-element.29.refs_4_), channel_id=1, source_target_pairs={{0,2},{1,3},{2,0},{3,1},{4,6},{5,7},{6,4},{7,5},{8,10},{9,11},{10,... | collective-permute-start | bytes 589832 | tf_op jit(solution)/shard_map/ppermute | solution.py:23
  41.0 0.5 collective-permute-start.8
  41.5 5.4 %shard_map.88 = (f32[32,3072]{1,0:T(8,128)S(1)}, f32[32,3072]{1,0:T(8,128)S(1)}, bf16[3072,3072]{1,0:T(8,128)(2,1)S(1)}) custom-call(s32[1]{0:T(128)} %bitcast.3.core_ref.refs_0_, bf16[192,1536]{1,0:T(8,128)(2,1)S(1)} %bitcast.15, bf16[192,1536]{1,0:T(8,128)(2,1)S(1)} %bitcast.17, ...), custom_call_target="tpu_custom_call", output_to_operand_aliasing={{2}: (3, {})} | custom-call | flops 1207959552 | bytes 18874368 | tf_op jit(solution)/shard_map/pallas_call | solution.py:47
  47.2 3.4 %collective-permute-done.8 = bf16[32,3072]{1,0:T(8,128)(2,1)S(1)} collective-permute-done((bf16[32,3072]{1,0:T(8,128)(2,1)S(1)}, bf16[32,3072]{1,0:T(8,128)(2,1)S(1)}, u32[]{:S(2)}, u32[]{:S(2)}) %collective-permute-start.8) | collective-permute-done | bytes 196640 | tf_op jit(solution)/shard_map/ppermute | solution.py:23
  50.6 0.3 fusion.3
  51.0 1.6 %collective-permute-start.12 = (bf16[32,3072]{1,0:T(8,128)(2,1)S(1)}, bf16[32,3072]{1,0:T(8,128)(2,1)S(1)}, u32[]{:S(2)}, u32[]{:S(2)}) collective-permute-start(bf16[32,3072]{1,0:T(8,128)(2,1)S(1)} %get-tuple-element.46.refs_4_), channel_id=1, source_target_pairs={{0,2},{1,3},{2,0},{3,1},{4,6},{5,7},{6,4},{7,5},{8,10},{9,11},{10,... | collective-permute-start | bytes 589832 | tf_op jit(solution)/shard_map/ppermute | solution.py:23
  52.7 4.5 %collective-permute-done.12 = bf16[32,3072]{1,0:T(8,128)(2,1)S(1)} collective-permute-done((bf16[32,3072]{1,0:T(8,128)(2,1)S(1)}, bf16[32,3072]{1,0:T(8,128)(2,1)S(1)}, u32[]{:S(2)}, u32[]{:S(2)}) %collective-permute-start.12) | collective-permute-done | bytes 196640 | tf_op jit(solution)/shard_map/ppermute | solution.py:23
  57.4 3.1 %shard_map.89 = (f32[32,3072]{1,0:T(8,128)S(1)}, bf16[32,3072]{1,0:T(8,128)(2,1)S(1)}) custom-call(s32[1]{0:T(128)} %bitcast.3.core_ref.refs_0_, bf16[32,3072]{1,0:T(8,128)(2,1)S(1)} %get-tuple-element.59.refs_1_, bf16[32,3072]{1,0:T(8,128)(2,1)S(1)} %get-tuple-element.60.refs_2_, bf16[3072,3072]{1,0:T(8,128)(2,1)S(1)} %get-tuple-element.34.refs_3_, ...), custom_call_target="tpu_custom_call" | custom-call | flops 1207959552 | bytes 18874368 | tf_op jit(solution)/shard_map/pallas_call | solution.py:47
  60.5 0.6 collective-permute-start.11
  61.2 5.7 %shard_map.90 = (f32[32,3072]{1,0:T(8,128)S(1)}, bf16[32,3072]{1,0:T(8,128)(2,1)S(1)}) custom-call(s32[1]{0:T(128)} %bitcast.3.core_ref.refs_0_, bf16[32,3072]{1,0:T(8,128)(2,1)S(1)} %multiply_convert_fusion.refs_1_, bf16[32,3072]{1,0:T(8,128)(2,1)S(1)} %collective-permute-done.13.refs_2_, bf16[3072,3072]{1,0:T(8,128)(2,1)S(1)} %get-tuple-element.40.refs_3_, ...), custom_call_target="tpu_custom_call" | custom-call | flops 1207959552 | bytes 18874368 | tf_op jit(solution)/shard_map/pallas_call | solution.py:47
  66.8 1.6 %collective-permute-start.14 = (bf16[32,3072]{1,0:T(8,128)(2,1)S(1)}, bf16[32,3072]{1,0:T(8,128)(2,1)S(1)}, u32[]{:S(2)}, u32[]{:S(2)}) collective-permute-start(bf16[32,3072]{1,0:T(8,128)(2,1)S(1)} %get-tuple-element.42.refs_2_), channel_id=1, source_target_pairs={{0,4},{4,0},{8,12},{12,8},{16,20},{20,16},{24,28},{28,24},{1,5},{5... | collective-permute-start | bytes 589832 | tf_op jit(solution)/shard_map/ppermute | solution.py:23
  68.5 5.4 %collective-permute-done.14 = bf16[32,3072]{1,0:T(8,128)(2,1)S(1)} collective-permute-done((bf16[32,3072]{1,0:T(8,128)(2,1)S(1)}, bf16[32,3072]{1,0:T(8,128)(2,1)S(1)}, u32[]{:S(2)}, u32[]{:S(2)}) %collective-permute-start.14) | collective-permute-done | bytes 196640 | tf_op jit(solution)/shard_map/ppermute | solution.py:23
  74.0 1.8 %collective-permute-start.15 = (bf16[16,6144]{1,0:T(8,128)(2,1)S(1)}, bf16[16,6144]{1,0:T(8,128)(2,1)S(1)}, u32[]{:S(2)}, u32[]{:S(2)}) collective-permute-start(bf16[16,6144]{1,0:T(8,128)(2,1)S(1)} %fusion.6.refs_5_), channel_id=1, source_target_pairs={{0,8},{4,12},{8,0},{12,4},{16,24},{20,28},{24,16},{28,20},{1,9},{5... | collective-permute-start | bytes 589832 | tf_op jit(solution)/shard_map/ppermute | solution.py:23
  75.8 5.8 %shard_map.91.refs_4_ = bf16[3072,3072]{1,0:T(8,128)(2,1)} custom-call(bf16[64,3072]{1,0:T(8,128)(2,1)S(1)} %pad_maximum_fusion.5.refs_0_, bf16[64,3072]{1,0:T(8,128)(2,1)S(1)} %pad_maximum_fusion.6.refs_1_, bf16[32,3072]{1,0:T(8,128)(2,1)S(1)} %get-tuple-element.42.refs_2_), custom_call_target="tpu_custom_call" | custom-call | flops 805306368 | bytes 12582912 | tf_op jit(solution)/shard_map/pallas_call | solution.py:47
  81.7 1.7 %collective-permute-start.16 = (bf16[8,6144]{1,0:T(8,128)(2,1)S(1)}, bf16[8,6144]{1,0:T(8,128)(2,1)S(1)}, u32[]{:S(2)}, u32[]{:S(2)}) collective-permute-start(bf16[8,6144]{1,0:T(8,128)(2,1)S(1)} %slice.179.refs_3_), channel_id=1, source_target_pairs={{0,16},{4,20},{8,24},{12,28},{16,0},{20,4},{24,8},{28,12},{1,17},{... | collective-permute-start | bytes 294920 | tf_op jit(solution)/shard_map/ppermute | solution.py:23
  83.4 5.8 %shard_map.92 = (bf16[3072,3072]{1,0:T(8,128)(2,1)}, bf16[3072,3072]{1,0:T(8,128)(2,1)}) custom-call(bf16[64,3072]{1,0:T(8,128)(2,1)S(1)} %pad_maximum_fusion.5.refs_0_, bf16[64,3072]{1,0:T(8,128)(2,1)S(1)} %pad_maximum_fusion.6.refs_1_, bf16[64,3072]{1,0:T(8,128)(2,1)S(1)} %get-tuple-element.68.refs_2_.refs_0_, ...), custom_call_target="tpu_custom_call", output_to_operand_aliasing={{0}: (4, {})} | custom-call | flops 805306368 | bytes 12582912 | tf_op jit(solution)/shard_map/pallas_call | solution.py:47
  89.1 5.8 %shard_map.93 = bf16[3072,3072]{1,0:T(8,128)(2,1)} custom-call(bf16[64,3072]{1,0:T(8,128)(2,1)S(1)} %get-tuple-element.68.refs_2_.refs_0_, bf16[64,3072]{1,0:T(8,128)(2,1)S(1)} %get-tuple-element.69.refs_3_.refs_1_, bf16[3072,3072]{1,0:T(8,128)(2,1)} %get-tuple-element.44.refs_2_, bf16[8,6144]{1,0:T(8,128)(2,1)S(1)} %slice.179.refs_3_), custom_call_target="tpu_custom_call", output_to_operand_aliasing={{}: (2, {})} | custom-call | flops 805306368 | bytes 12582912 | tf_op jit(solution)/shard_map/pallas_call | solution.py:47
  95.0 0.6 fusion.11
  (46 shorter events, 1.5 us)
Async XLA Ops:
  1.5 9.4 %collective-permute-start.3 = (bf16[3,8,1536]{2,1,0:T(8,128)(2,1)S(1)}, bf16[3,8,1536]{2,1,0:T(8,128)(2,1)S(1)}, u32[]{:S(2)}, u32[]{:S(2)}) collective-permute-start(bf16[3,8,1536]{2,1,0:T(8,128)(2,1)S(1)} %get-tuple-element.63.refs_1_), channel_id=1, source_target_pairs={{0,4},{4,0},{8,12},{12,8},{16,20},{20,16},{24,28},{28,24},{1,5},{5... | collective-permute-start | bytes 221192 | tf_op jit(solution)/shard_map/ppermute | solution.py:23
  4.6 6.8 %collective-permute-start = (bf16[3,8,1536]{2,1,0:T(8,128)(2,1)S(1)}, bf16[3,8,1536]{2,1,0:T(8,128)(2,1)S(1)}, u32[]{:S(2)}, u32[]{:S(2)}) collective-permute-start(bf16[3,8,1536]{2,1,0:T(8,128)(2,1)S(1)} %get-tuple-element.65), channel_id=1, source_target_pairs={{0,16},{4,20},{8,24},{12,28},{16,0},{20,4},{24,8},{28,12},{1,17},{... | collective-permute-start | bytes 221192 | tf_op jit(solution)/shard_map/ppermute | solution.py:23
  11.0 9.2 %collective-permute-start.4 = (bf16[3,16,1536]{2,1,0:T(8,128)(2,1)S(1)}, bf16[3,16,1536]{2,1,0:T(8,128)(2,1)S(1)}, u32[]{:S(2)}, u32[]{:S(2)}) collective-permute-start(bf16[3,16,1536]{2,1,0:T(8,128)(2,1)S(1)} %pad_maximum_fusion.11.refs_2_), channel_id=1, source_target_pairs={{0,16},{4,20},{8,24},{12,28},{16,0},{20,4},{24,8},{28,12},{1,17},{... | collective-permute-start | bytes 442376 | tf_op jit(solution)/shard_map/ppermute | solution.py:23
  11.4 15.4 %collective-permute-start.1 = (bf16[3,16,1536]{2,1,0:T(8,128)(2,1)S(1)}, bf16[3,16,1536]{2,1,0:T(8,128)(2,1)S(1)}, u32[]{:S(2)}, u32[]{:S(2)}) collective-permute-start(bf16[3,16,1536]{2,1,0:T(8,128)(2,1)S(1)} %pad_maximum_fusion.10), channel_id=1, source_target_pairs={{0,8},{4,12},{8,0},{12,4},{16,24},{20,28},{24,16},{28,20},{1,9},{5... | collective-permute-start | bytes 442376 | tf_op jit(solution)/shard_map/ppermute | solution.py:23
  20.2 7.4 %collective-permute-start.5 = (bf16[3,32,1536]{2,1,0:T(8,128)(2,1)S(1)}, bf16[3,32,1536]{2,1,0:T(8,128)(2,1)S(1)}, u32[]{:S(2)}, u32[]{:S(2)}) collective-permute-start(bf16[3,32,1536]{2,1,0:T(8,128)(2,1)S(1)} %pad_maximum_fusion.8.refs_1_), channel_id=1, source_target_pairs={{0,8},{4,12},{8,0},{12,4},{16,24},{20,28},{24,16},{28,20},{1,9},{5... | collective-permute-start | bytes 884744 | tf_op jit(solution)/shard_map/ppermute | solution.py:23
  26.9 7.4 %collective-permute-start.2 = (bf16[3,32,1536]{2,1,0:T(8,128)(2,1)S(1)}, bf16[3,32,1536]{2,1,0:T(8,128)(2,1)S(1)}, u32[]{:S(2)}, u32[]{:S(2)}) collective-permute-start(bf16[3,32,1536]{2,1,0:T(8,128)(2,1)S(1)} %pad_maximum_fusion.7), channel_id=1, source_target_pairs={{0,4},{4,0},{8,12},{12,8},{16,20},{20,16},{24,28},{28,24},{1,5},{5... | collective-permute-start | bytes 884744 | tf_op jit(solution)/shard_map/ppermute | solution.py:23
  37.5 1.8 %collective-permute-start.6 = (bf16[64,3072]{1,0:T(8,128)(2,1)S(1)}, bf16[64,3072]{1,0:T(8,128)(2,1)S(1)}, u32[]{:S(2)}, u32[]{:S(2)}) collective-permute-start(bf16[64,3072]{1,0:T(8,128)(2,1)S(1)} %get-tuple-element.28), channel_id=1, source_target_pairs={{0,1},{1,0},{2,3},{3,2},{4,5},{5,4},{6,7},{7,6},{8,9},{9,8},{10,11... | collective-permute-start | bytes 1179656 | tf_op jit(solution)/shard_map/ppermute | solution.py:23
  39.4 7.8 %collective-permute-start.7 = (bf16[32,3072]{1,0:T(8,128)(2,1)S(1)}, bf16[32,3072]{1,0:T(8,128)(2,1)S(1)}, u32[]{:S(2)}, u32[]{:S(2)}) collective-permute-start(bf16[32,3072]{1,0:T(8,128)(2,1)S(1)} %get-tuple-element.29.refs_4_), channel_id=1, source_target_pairs={{0,2},{1,3},{2,0},{3,1},{4,6},{5,7},{6,4},{7,5},{8,10},{9,11},{10,... | collective-permute-start | bytes 589832 | tf_op jit(solution)/shard_map/ppermute | solution.py:23
  41.0 9.6 %collective-permute-start.8 = (bf16[32,3072]{1,0:T(8,128)(2,1)S(1)}, bf16[32,3072]{1,0:T(8,128)(2,1)S(1)}, u32[]{:S(2)}, u32[]{:S(2)}) collective-permute-start(bf16[32,3072]{1,0:T(8,128)(2,1)S(1)} %get-tuple-element.30), channel_id=1, source_target_pairs={{0,2},{1,3},{2,0},{3,1},{4,6},{5,7},{6,4},{7,5},{8,10},{9,11},{10,... | collective-permute-start | bytes 589832 | tf_op jit(solution)/shard_map/ppermute | solution.py:23
  47.0 4.0 %collective-permute-start.10 = (f32[32,3072]{1,0:T(8,128)S(1)}, f32[32,3072]{1,0:T(8,128)S(1)}, u32[]{:S(2)}, u32[]{:S(2)}) collective-permute-start(f32[32,3072]{1,0:T(8,128)S(1)} %get-tuple-element.36), channel_id=1, source_target_pairs={{0,1},{1,0},{2,3},{3,2},{4,5},{5,4},{6,7},{7,6},{8,9},{9,8},{10,11... | collective-permute-start | bytes 1179656 | tf_op jit(solution)/shard_map/ppermute | solution.py:23
  51.0 6.2 %collective-permute-start.12 = (bf16[32,3072]{1,0:T(8,128)(2,1)S(1)}, bf16[32,3072]{1,0:T(8,128)(2,1)S(1)}, u32[]{:S(2)}, u32[]{:S(2)}) collective-permute-start(bf16[32,3072]{1,0:T(8,128)(2,1)S(1)} %get-tuple-element.46.refs_4_), channel_id=1, source_target_pairs={{0,2},{1,3},{2,0},{3,1},{4,6},{5,7},{6,4},{7,5},{8,10},{9,11},{10,... | collective-permute-start | bytes 589832 | tf_op jit(solution)/shard_map/ppermute | solution.py:23
  52.6 4.7 %collective-permute-start.9 = (bf16[64,3072]{1,0:T(8,128)(2,1)S(1)}, bf16[64,3072]{1,0:T(8,128)(2,1)S(1)}, u32[]{:S(2)}, u32[]{:S(2)}) collective-permute-start(bf16[64,3072]{1,0:T(8,128)(2,1)S(1)} %pad_maximum_fusion.2), channel_id=1, source_target_pairs={{0,1},{1,0},{2,3},{3,2},{4,5},{5,4},{6,7},{7,6},{8,9},{9,8},{10,11... | collective-permute-start | bytes 1179656 | tf_op jit(solution)/shard_map/ppermute | solution.py:23
  57.2 3.9 %collective-permute-start.13 = (bf16[32,3072]{1,0:T(8,128)(2,1)S(1)}, bf16[32,3072]{1,0:T(8,128)(2,1)S(1)}, u32[]{:S(2)}, u32[]{:S(2)}) collective-permute-start(bf16[32,3072]{1,0:T(8,128)(2,1)S(1)} %multiply_convert_fusion.refs_1_), channel_id=1, source_target_pairs={{0,1},{1,0},{2,3},{3,2},{4,5},{5,4},{6,7},{7,6},{8,9},{9,8},{10,11... | collective-permute-start | bytes 589832 | tf_op jit(solution)/shard_map/ppermute | solution.py:23
  60.5 7.9 %collective-permute-start.11 = (bf16[32,3072]{1,0:T(8,128)(2,1)S(1)}, bf16[32,3072]{1,0:T(8,128)(2,1)S(1)}, u32[]{:S(2)}, u32[]{:S(2)}) collective-permute-start(bf16[32,3072]{1,0:T(8,128)(2,1)S(1)} %get-tuple-element.38.refs_4_), channel_id=1, source_target_pairs={{0,4},{4,0},{8,12},{12,8},{16,20},{20,16},{24,28},{28,24},{1,5},{5... | collective-permute-start | bytes 589832 | tf_op jit(solution)/shard_map/ppermute | solution.py:23
  66.8 7.1 %collective-permute-start.14 = (bf16[32,3072]{1,0:T(8,128)(2,1)S(1)}, bf16[32,3072]{1,0:T(8,128)(2,1)S(1)}, u32[]{:S(2)}, u32[]{:S(2)}) collective-permute-start(bf16[32,3072]{1,0:T(8,128)(2,1)S(1)} %get-tuple-element.42.refs_2_), channel_id=1, source_target_pairs={{0,4},{4,0},{8,12},{12,8},{16,20},{20,16},{24,28},{28,24},{1,5},{5... | collective-permute-start | bytes 589832 | tf_op jit(solution)/shard_map/ppermute | solution.py:23
  74.0 7.6 %collective-permute-start.15 = (bf16[16,6144]{1,0:T(8,128)(2,1)S(1)}, bf16[16,6144]{1,0:T(8,128)(2,1)S(1)}, u32[]{:S(2)}, u32[]{:S(2)}) collective-permute-start(bf16[16,6144]{1,0:T(8,128)(2,1)S(1)} %fusion.6.refs_5_), channel_id=1, source_target_pairs={{0,8},{4,12},{8,0},{12,4},{16,24},{20,28},{24,16},{28,20},{1,9},{5... | collective-permute-start | bytes 589832 | tf_op jit(solution)/shard_map/ppermute | solution.py:23
  81.7 13.2 %collective-permute-start.16 = (bf16[8,6144]{1,0:T(8,128)(2,1)S(1)}, bf16[8,6144]{1,0:T(8,128)(2,1)S(1)}, u32[]{:S(2)}, u32[]{:S(2)}) collective-permute-start(bf16[8,6144]{1,0:T(8,128)(2,1)S(1)} %slice.179.refs_3_), channel_id=1, source_target_pairs={{0,16},{4,20},{8,24},{12,28},{16,0},{20,4},{24,8},{28,12},{1,17},{... | collective-permute-start | bytes 294920 | tf_op jit(solution)/shard_map/ppermute | solution.py:23

commit v4 on v3

--- a/solution.py
+++ b/solution.py
@@ -123,7 +123,7 @@
     h = x.shape[1]
     first, count, groups = rows
     tall = count // groups // 2
-    b = block_of(n, 1024 if here else 512)
+    b = block_of(n, 3072 if free == 1 else 1536)
 
     def kernel(core_ref, x_ref, y_ref, w_ref, mine_ref, send_ref, held, *sems):
         one = pl.ds(first, count)
@@ -172,7 +172,7 @@
     k, n = w.shape[dims[1][0]], w.shape[free]
     half = own.shape[0]
     tall = max(2 * half, 128 if free == 1 else 0)
-    b = block_of(n, 1024 if here else 512)
+    b = block_of(n, 3072 if free == 1 else 1536)
 
     def kernel(core_ref, own_ref, other_ref, w_ref, keep_ref, send_ref, x_ref, *scratch):
         low = core_ref[0] == 0
@@ -221,11 +221,8 @@
     tall = max(b for _, _, b in blocks)
     depth, width = jobs[0][1].shape
     count = len(jobs)
-    sizes = [width]
-    while len(sizes) < 4 and sizes[-1] % 256 == 0:
-        sizes[-1:] = [sizes[-1] // 2] * 2
-    cuts = [sizes[::-1]] + [sizes[:1] + [width - sizes[0]]] * (len(blocks) - 2) + [sizes]
-    columns = [[(sum(cut[:i]), n) for i, n in enumerate(cut) if n] for cut in cuts[-len(blocks) :]]
+    wide = block_of(width, 512)
+    columns = [[(c, wide) for c in range(0, width, wide)] for _ in blocks]
 
     def kernel(*refs):
         sides = refs[: 2 * count]

time: 95.8 us -> 93.6 us (0.977)
  Pallas kernels: 48.8 us -> 45.9 us
    pallas_call x10, Pallas kernels: 48.8 us -> 45.9 us  [call(): pl.pallas_call(body, in_specs=in_specs, out_specs=out_specs, out_shape=ou...]
  transfers between devices with their start and end apart: 17 -> 17, of which waited for: 8 -> 8; matrix products, arithmetic and copies ran while one was open for 1% -> 1% of each run, Pallas kernels for 48% -> 46%
where the time goes in v4:
time: 93.6 us; the launch traced here: 93.4 us
  Pallas kernels  45.9 us (49%)
  waiting for transfers between devices  25.3 us (27%)
  starting transfers between devices  18.5 us (20%)
  other arithmetic  1.87 us (2%)
  between operations  0.99 us (1%)
    pallas_call x10, Pallas kernels, call(): pl.pallas_call(body, in_specs=in_specs, out_specs=out_specs, out_shape=ou...  45.9 us
    ppermute x17, waiting for transfers between devices, swap(): return lax.ppermute(x, axis, [(i, i ^ bit) for i in range(n)])  25.3 us
    ppermute x17, starting transfers between devices, swap(): return lax.ppermute(x, axis, [(i, i ^ bit) for i in range(n)])  18.5 us
  transfers between devices with their start and end apart: 17, of which 8 were waited for; matrix products, arithmetic and copies ran while one was open for 1% of the time, Pallas kernels for 46%

profile of v4, /device:TPU:0, one launch (start us, length us, event | category | flops | bytes accessed | tf_op | source)
XLA Modules:
  0.0 93.4 jit_solution(6566171172132642347)
XLA Ops:
  0.6 0.9 pad_maximum_fusion.9
  1.5 3.0 %collective-permute-start.3 = (bf16[3,8,1536]{2,1,0:T(8,128)(2,1)S(1)}, bf16[3,8,1536]{2,1,0:T(8,128)(2,1)S(1)}, u32[]{:S(2)}, u32[]{:S(2)}) collective-permute-start(bf16[3,8,1536]{2,1,0:T(8,128)(2,1)S(1)} %get-tuple-element.63.refs_1_), channel_id=1, source_target_pairs={{0,4},{4,0},{8,12},{12,8},{16,20},{20,16},{24,28},{28,24},{1,5},{5... | collective-permute-start | bytes 221192 | tf_op jit(solution)/shard_map/ppermute | solution.py:23
  4.6 2.6 %collective-permute-start = (bf16[3,8,1536]{2,1,0:T(8,128)(2,1)S(1)}, bf16[3,8,1536]{2,1,0:T(8,128)(2,1)S(1)}, u32[]{:S(2)}, u32[]{:S(2)}) collective-permute-start(bf16[3,8,1536]{2,1,0:T(8,128)(2,1)S(1)} %get-tuple-element.65), channel_id=1, source_target_pairs={{0,16},{4,20},{8,24},{12,28},{16,0},{20,4},{24,8},{28,12},{1,17},{... | collective-permute-start | bytes 221192 | tf_op jit(solution)/shard_map/ppermute | solution.py:23
  7.2 3.8 %shard_map.86.refs_1_ = bf16[3072,3072]{1,0:T(8,128)(2,1)S(1)} custom-call(bf16[3072,3072]{1,0:T(8,128)(2,1)} %refs_0_.5, bf16[3,8,1536]{2,1,0:T(8,128)(2,1)S(1)} %get-tuple-element.63.refs_1_), custom_call_target="tpu_custom_call" | custom-call | flops 603979776 | bytes 9437184 | tf_op jit(solution)/shard_map/pallas_call | solution.py:47
  11.0 0.4 collective-permute-start.4
  11.4 1.6 %collective-permute-start.1 = (bf16[3,16,1536]{2,1,0:T(8,128)(2,1)S(1)}, bf16[3,16,1536]{2,1,0:T(8,128)(2,1)S(1)}, u32[]{:S(2)}, u32[]{:S(2)}) collective-permute-start(bf16[3,16,1536]{2,1,0:T(8,128)(2,1)S(1)} %pad_maximum_fusion.10), channel_id=1, source_target_pairs={{0,8},{4,12},{8,0},{12,4},{16,24},{20,28},{24,16},{28,20},{1,9},{5... | collective-permute-start | bytes 442376 | tf_op jit(solution)/shard_map/ppermute | solution.py:23
  13.1 3.8 %shard_map.87.refs_3_ = bf16[3072,3072]{1,0:T(8,128)(2,1)S(1)} custom-call(bf16[3072,3072]{1,0:T(8,128)(2,1)} %refs_0_.5, bf16[3072,3072]{1,0:T(8,128)(2,1)S(1)} %shard_map.86.refs_1_, bf16[3,16,1536]{2,1,0:T(8,128)(2,1)S(1)} %pad_maximum_fusion.11.refs_2_), custom_call_target="tpu_custom_call", output_to_operand_aliasing={{}: (1, {})} | custom-call | flops 603979776 | bytes 9437184 | tf_op jit(solution)/shard_map/pallas_call | solution.py:47
  16.9 3.3 %collective-permute-done.4 = bf16[3,16,1536]{2,1,0:T(8,128)(2,1)S(1)} collective-permute-done((bf16[3,16,1536]{2,1,0:T(8,128)(2,1)S(1)}, bf16[3,16,1536]{2,1,0:T(8,128)(2,1)S(1)}, u32[]{:S(2)}, u32[]{:S(2)}) %collective-permute-start.4) | collective-permute-done | bytes 147488 | tf_op jit(solution)/shard_map/ppermute | solution.py:23
  20.3 6.5 %shard_map.84.w_ref = bf16[3072,3072]{1,0:T(8,128)(2,1)S(1)} custom-call(bf16[3072,3072]{1,0:T(8,128)(2,1)} %refs_0_.3, bf16[3,32,1536]{2,1,0:T(8,128)(2,1)S(1)} %pad_maximum_fusion.8.refs_1_), custom_call_target="tpu_custom_call" | custom-call | flops 1207959552 | bytes 18874368 | tf_op jit(solution)/shard_map/pallas_call | solution.py:47
  26.9 0.6 collective-permute-start.2
  27.8 6.5 %collective-permute-done.2 = bf16[3,32,1536]{2,1,0:T(8,128)(2,1)S(1)} collective-permute-done((bf16[3,32,1536]{2,1,0:T(8,128)(2,1)S(1)}, bf16[3,32,1536]{2,1,0:T(8,128)(2,1)S(1)}, u32[]{:S(2)}, u32[]{:S(2)}) %collective-permute-start.2) | collective-permute-done | bytes 294944 | tf_op jit(solution)/shard_map/ppermute | solution.py:23
  34.4 2.8 %shard_map.85 = (f32[64,3072]{1,0:T(8,128)S(1)}, bf16[64,3072]{1,0:T(8,128)(2,1)S(1)}, bf16[3072,3072]{1,0:T(8,128)(2,1)S(1)}) custom-call(s32[1]{0:T(128)} %bitcast.3.core_ref.refs_0_, bf16[192,1536]{1,0:T(8,128)(2,1)S(1)} %bitcast.14, bf16[192,1536]{1,0:T(8,128)(2,1)S(1)} %bitcast.16, ...), custom_call_target="tpu_custom_call", output_to_operand_aliasing={{2}: (3, {})} | custom-call | flops 1207959552 | bytes 18874368 | tf_op jit(solution)/shard_map/pallas_call | solution.py:47
  37.3 1.7 %collective-permute-done.6 = bf16[64,3072]{1,0:T(8,128)(2,1)S(1)} collective-permute-done((bf16[64,3072]{1,0:T(8,128)(2,1)S(1)}, bf16[64,3072]{1,0:T(8,128)(2,1)S(1)}, u32[]{:S(2)}, u32[]{:S(2)}) %collective-permute-start.6) | collective-permute-done | bytes 393248 | tf_op jit(solution)/shard_map/ppermute | solution.py:23
  39.1 1.6 %collective-permute-start.7 = (bf16[32,3072]{1,0:T(8,128)(2,1)S(1)}, bf16[32,3072]{1,0:T(8,128)(2,1)S(1)}, u32[]{:S(2)}, u32[]{:S(2)}) collective-permute-start(bf16[32,3072]{1,0:T(8,128)(2,1)S(1)} %get-tuple-element.29.refs_4_), channel_id=1, source_target_pairs={{0,2},{1,3},{2,0},{3,1},{4,6},{5,7},{6,4},{7,5},{8,10},{9,11},{10,... | collective-permute-start | bytes 589832 | tf_op jit(solution)/shard_map/ppermute | solution.py:23
  40.6 0.5 collective-permute-start.8
  41.2 5.4 %shard_map.88 = (f32[32,3072]{1,0:T(8,128)S(1)}, f32[32,3072]{1,0:T(8,128)S(1)}, bf16[3072,3072]{1,0:T(8,128)(2,1)S(1)}) custom-call(s32[1]{0:T(128)} %bitcast.3.core_ref.refs_0_, bf16[192,1536]{1,0:T(8,128)(2,1)S(1)} %bitcast.15, bf16[192,1536]{1,0:T(8,128)(2,1)S(1)} %bitcast.17, ...), custom_call_target="tpu_custom_call", output_to_operand_aliasing={{2}: (3, {})} | custom-call | flops 1207959552 | bytes 18874368 | tf_op jit(solution)/shard_map/pallas_call | solution.py:47
  46.6 0.3 collective-permute-done.7
  46.9 3.4 %collective-permute-done.8 = bf16[32,3072]{1,0:T(8,128)(2,1)S(1)} collective-permute-done((bf16[32,3072]{1,0:T(8,128)(2,1)S(1)}, bf16[32,3072]{1,0:T(8,128)(2,1)S(1)}, u32[]{:S(2)}, u32[]{:S(2)}) %collective-permute-start.8) | collective-permute-done | bytes 196640 | tf_op jit(solution)/shard_map/ppermute | solution.py:23
  50.3 0.3 fusion.3
  50.7 1.6 %collective-permute-start.12 = (bf16[32,3072]{1,0:T(8,128)(2,1)S(1)}, bf16[32,3072]{1,0:T(8,128)(2,1)S(1)}, u32[]{:S(2)}, u32[]{:S(2)}) collective-permute-start(bf16[32,3072]{1,0:T(8,128)(2,1)S(1)} %get-tuple-element.46.refs_4_), channel_id=1, source_target_pairs={{0,2},{1,3},{2,0},{3,1},{4,6},{5,7},{6,4},{7,5},{8,10},{9,11},{10,... | collective-permute-start | bytes 589832 | tf_op jit(solution)/shard_map/ppermute | solution.py:23
  52.3 4.5 %collective-permute-done.12 = bf16[32,3072]{1,0:T(8,128)(2,1)S(1)} collective-permute-done((bf16[32,3072]{1,0:T(8,128)(2,1)S(1)}, bf16[32,3072]{1,0:T(8,128)(2,1)S(1)}, u32[]{:S(2)}, u32[]{:S(2)}) %collective-permute-start.12) | collective-permute-done | bytes 196640 | tf_op jit(solution)/shard_map/ppermute | solution.py:23
  57.1 2.7 %shard_map.89 = (f32[32,3072]{1,0:T(8,128)S(1)}, bf16[32,3072]{1,0:T(8,128)(2,1)S(1)}) custom-call(s32[1]{0:T(128)} %bitcast.3.core_ref.refs_0_, bf16[32,3072]{1,0:T(8,128)(2,1)S(1)} %get-tuple-element.59.refs_1_, bf16[32,3072]{1,0:T(8,128)(2,1)S(1)} %get-tuple-element.60.refs_2_, bf16[3072,3072]{1,0:T(8,128)(2,1)S(1)} %get-tuple-element.34.refs_3_, ...), custom_call_target="tpu_custom_call" | custom-call | flops 1207959552 | bytes 18874368 | tf_op jit(solution)/shard_map/pallas_call | solution.py:47
  59.7 0.6 collective-permute-start.11
  60.3 5.6 %shard_map.90 = (f32[32,3072]{1,0:T(8,128)S(1)}, bf16[32,3072]{1,0:T(8,128)(2,1)S(1)}) custom-call(s32[1]{0:T(128)} %bitcast.3.core_ref.refs_0_, bf16[32,3072]{1,0:T(8,128)(2,1)S(1)} %multiply_convert_fusion.refs_1_, bf16[32,3072]{1,0:T(8,128)(2,1)S(1)} %collective-permute-done.13.refs_2_, bf16[3072,3072]{1,0:T(8,128)(2,1)S(1)} %get-tuple-element.40.refs_3_, ...), custom_call_target="tpu_custom_call" | custom-call | flops 1207959552 | bytes 18874368 | tf_op jit(solution)/shard_map/pallas_call | solution.py:47
  65.9 1.6 %collective-permute-start.14 = (bf16[32,3072]{1,0:T(8,128)(2,1)S(1)}, bf16[32,3072]{1,0:T(8,128)(2,1)S(1)}, u32[]{:S(2)}, u32[]{:S(2)}) collective-permute-start(bf16[32,3072]{1,0:T(8,128)(2,1)S(1)} %get-tuple-element.42.refs_2_), channel_id=1, source_target_pairs={{0,4},{4,0},{8,12},{12,8},{16,20},{20,16},{24,28},{28,24},{1,5},{5... | collective-permute-start | bytes 589832 | tf_op jit(solution)/shard_map/ppermute | solution.py:23
  67.6 5.4 %collective-permute-done.14 = bf16[32,3072]{1,0:T(8,128)(2,1)S(1)} collective-permute-done((bf16[32,3072]{1,0:T(8,128)(2,1)S(1)}, bf16[32,3072]{1,0:T(8,128)(2,1)S(1)}, u32[]{:S(2)}, u32[]{:S(2)}) %collective-permute-start.14) | collective-permute-done | bytes 196640 | tf_op jit(solution)/shard_map/ppermute | solution.py:23
  73.1 1.8 %collective-permute-start.15 = (bf16[16,6144]{1,0:T(8,128)(2,1)S(1)}, bf16[16,6144]{1,0:T(8,128)(2,1)S(1)}, u32[]{:S(2)}, u32[]{:S(2)}) collective-permute-start(bf16[16,6144]{1,0:T(8,128)(2,1)S(1)} %fusion.6.refs_5_), channel_id=1, source_target_pairs={{0,8},{4,12},{8,0},{12,4},{16,24},{20,28},{24,16},{28,20},{1,9},{5... | collective-permute-start | bytes 589832 | tf_op jit(solution)/shard_map/ppermute | solution.py:23
  74.9 5.1 %shard_map.91.refs_4_ = bf16[3072,3072]{1,0:T(8,128)(2,1)} custom-call(bf16[64,3072]{1,0:T(8,128)(2,1)S(1)} %pad_maximum_fusion.5.refs_0_, bf16[64,3072]{1,0:T(8,128)(2,1)S(1)} %pad_maximum_fusion.6.refs_1_, bf16[32,3072]{1,0:T(8,128)(2,1)S(1)} %get-tuple-element.42.refs_2_), custom_call_target="tpu_custom_call" | custom-call | flops 805306368 | bytes 12582912 | tf_op jit(solution)/shard_map/pallas_call | solution.py:47
  80.1 2.3 %collective-permute-start.16 = (bf16[8,6144]{1,0:T(8,128)(2,1)S(1)}, bf16[8,6144]{1,0:T(8,128)(2,1)S(1)}, u32[]{:S(2)}, u32[]{:S(2)}) collective-permute-start(bf16[8,6144]{1,0:T(8,128)(2,1)S(1)} %slice.179.refs_3_), channel_id=1, source_target_pairs={{0,16},{4,20},{8,24},{12,28},{16,0},{20,4},{24,8},{28,12},{1,17},{... | collective-permute-start | bytes 294920 | tf_op jit(solution)/shard_map/ppermute | solution.py:23
  82.4 5.1 %shard_map.92 = (bf16[3072,3072]{1,0:T(8,128)(2,1)}, bf16[3072,3072]{1,0:T(8,128)(2,1)}) custom-call(bf16[64,3072]{1,0:T(8,128)(2,1)S(1)} %pad_maximum_fusion.5.refs_0_, bf16[64,3072]{1,0:T(8,128)(2,1)S(1)} %pad_maximum_fusion.6.refs_1_, bf16[64,3072]{1,0:T(8,128)(2,1)S(1)} %get-tuple-element.68.refs_2_.refs_0_, ...), custom_call_target="tpu_custom_call", output_to_operand_aliasing={{0}: (4, {})} | custom-call | flops 805306368 | bytes 12582912 | tf_op jit(solution)/shard_map/pallas_call | solution.py:47
  87.6 5.1 %shard_map.93 = bf16[3072,3072]{1,0:T(8,128)(2,1)} custom-call(bf16[64,3072]{1,0:T(8,128)(2,1)S(1)} %get-tuple-element.68.refs_2_.refs_0_, bf16[64,3072]{1,0:T(8,128)(2,1)S(1)} %get-tuple-element.69.refs_3_.refs_1_, bf16[3072,3072]{1,0:T(8,128)(2,1)} %get-tuple-element.44.refs_2_, bf16[8,6144]{1,0:T(8,128)(2,1)S(1)} %slice.179.refs_3_), custom_call_target="tpu_custom_call", output_to_operand_aliasing={{}: (2, {})} | custom-call | flops 805306368 | bytes 12582912 | tf_op jit(solution)/shard_map/pallas_call | solution.py:47
  92.8 0.6 fusion.11
  (46 shorter events, 1.5 us)
Async XLA Ops:
  1.5 9.4 %collective-permute-start.3 = (bf16[3,8,1536]{2,1,0:T(8,128)(2,1)S(1)}, bf16[3,8,1536]{2,1,0:T(8,128)(2,1)S(1)}, u32[]{:S(2)}, u32[]{:S(2)}) collective-permute-start(bf16[3,8,1536]{2,1,0:T(8,128)(2,1)S(1)} %get-tuple-element.63.refs_1_), channel_id=1, source_target_pairs={{0,4},{4,0},{8,12},{12,8},{16,20},{20,16},{24,28},{28,24},{1,5},{5... | collective-permute-start | bytes 221192 | tf_op jit(solution)/shard_map/ppermute | solution.py:23
  4.6 6.8 %collective-permute-start = (bf16[3,8,1536]{2,1,0:T(8,128)(2,1)S(1)}, bf16[3,8,1536]{2,1,0:T(8,128)(2,1)S(1)}, u32[]{:S(2)}, u32[]{:S(2)}) collective-permute-start(bf16[3,8,1536]{2,1,0:T(8,128)(2,1)S(1)} %get-tuple-element.65), channel_id=1, source_target_pairs={{0,16},{4,20},{8,24},{12,28},{16,0},{20,4},{24,8},{28,12},{1,17},{... | collective-permute-start | bytes 221192 | tf_op jit(solution)/shard_map/ppermute | solution.py:23
  11.0 9.2 %collective-permute-start.4 = (bf16[3,16,1536]{2,1,0:T(8,128)(2,1)S(1)}, bf16[3,16,1536]{2,1,0:T(8,128)(2,1)S(1)}, u32[]{:S(2)}, u32[]{:S(2)}) collective-permute-start(bf16[3,16,1536]{2,1,0:T(8,128)(2,1)S(1)} %pad_maximum_fusion.11.refs_2_), channel_id=1, source_target_pairs={{0,16},{4,20},{8,24},{12,28},{16,0},{20,4},{24,8},{28,12},{1,17},{... | collective-permute-start | bytes 442376 | tf_op jit(solution)/shard_map/ppermute | solution.py:23
  11.4 15.4 %collective-permute-start.1 = (bf16[3,16,1536]{2,1,0:T(8,128)(2,1)S(1)}, bf16[3,16,1536]{2,1,0:T(8,128)(2,1)S(1)}, u32[]{:S(2)}, u32[]{:S(2)}) collective-permute-start(bf16[3,16,1536]{2,1,0:T(8,128)(2,1)S(1)} %pad_maximum_fusion.10), channel_id=1, source_target_pairs={{0,8},{4,12},{8,0},{12,4},{16,24},{20,28},{24,16},{28,20},{1,9},{5... | collective-permute-start | bytes 442376 | tf_op jit(solution)/shard_map/ppermute | solution.py:23
  20.2 7.4 %collective-permute-start.5 = (bf16[3,32,1536]{2,1,0:T(8,128)(2,1)S(1)}, bf16[3,32,1536]{2,1,0:T(8,128)(2,1)S(1)}, u32[]{:S(2)}, u32[]{:S(2)}) collective-permute-start(bf16[3,32,1536]{2,1,0:T(8,128)(2,1)S(1)} %pad_maximum_fusion.8.refs_1_), channel_id=1, source_target_pairs={{0,8},{4,12},{8,0},{12,4},{16,24},{20,28},{24,16},{28,20},{1,9},{5... | collective-permute-start | bytes 884744 | tf_op jit(solution)/shard_map/ppermute | solution.py:23
  26.9 7.4 %collective-permute-start.2 = (bf16[3,32,1536]{2,1,0:T(8,128)(2,1)S(1)}, bf16[3,32,1536]{2,1,0:T(8,128)(2,1)S(1)}, u32[]{:S(2)}, u32[]{:S(2)}) collective-permute-start(bf16[3,32,1536]{2,1,0:T(8,128)(2,1)S(1)} %pad_maximum_fusion.7), channel_id=1, source_target_pairs={{0,4},{4,0},{8,12},{12,8},{16,20},{20,16},{24,28},{28,24},{1,5},{5... | collective-permute-start | bytes 884744 | tf_op jit(solution)/shard_map/ppermute | solution.py:23
  37.2 1.8 %collective-permute-start.6 = (bf16[64,3072]{1,0:T(8,128)(2,1)S(1)}, bf16[64,3072]{1,0:T(8,128)(2,1)S(1)}, u32[]{:S(2)}, u32[]{:S(2)}) collective-permute-start(bf16[64,3072]{1,0:T(8,128)(2,1)S(1)} %get-tuple-element.28), channel_id=1, source_target_pairs={{0,1},{1,0},{2,3},{3,2},{4,5},{5,4},{6,7},{7,6},{8,9},{9,8},{10,11... | collective-permute-start | bytes 1179656 | tf_op jit(solution)/shard_map/ppermute | solution.py:23
  39.1 7.8 %collective-permute-start.7 = (bf16[32,3072]{1,0:T(8,128)(2,1)S(1)}, bf16[32,3072]{1,0:T(8,128)(2,1)S(1)}, u32[]{:S(2)}, u32[]{:S(2)}) collective-permute-start(bf16[32,3072]{1,0:T(8,128)(2,1)S(1)} %get-tuple-element.29.refs_4_), channel_id=1, source_target_pairs={{0,2},{1,3},{2,0},{3,1},{4,6},{5,7},{6,4},{7,5},{8,10},{9,11},{10,... | collective-permute-start | bytes 589832 | tf_op jit(solution)/shard_map/ppermute | solution.py:23
  40.6 9.7 %collective-permute-start.8 = (bf16[32,3072]{1,0:T(8,128)(2,1)S(1)}, bf16[32,3072]{1,0:T(8,128)(2,1)S(1)}, u32[]{:S(2)}, u32[]{:S(2)}) collective-permute-start(bf16[32,3072]{1,0:T(8,128)(2,1)S(1)} %get-tuple-element.30), channel_id=1, source_target_pairs={{0,2},{1,3},{2,0},{3,1},{4,6},{5,7},{6,4},{7,5},{8,10},{9,11},{10,... | collective-permute-start | bytes 589832 | tf_op jit(solution)/shard_map/ppermute | solution.py:23
  46.6 4.0 %collective-permute-start.10 = (f32[32,3072]{1,0:T(8,128)S(1)}, f32[32,3072]{1,0:T(8,128)S(1)}, u32[]{:S(2)}, u32[]{:S(2)}) collective-permute-start(f32[32,3072]{1,0:T(8,128)S(1)} %get-tuple-element.36), channel_id=1, source_target_pairs={{0,1},{1,0},{2,3},{3,2},{4,5},{5,4},{6,7},{7,6},{8,9},{9,8},{10,11... | collective-permute-start | bytes 1179656 | tf_op jit(solution)/shard_map/ppermute | solution.py:23
  50.7 6.2 %collective-permute-start.12 = (bf16[32,3072]{1,0:T(8,128)(2,1)S(1)}, bf16[32,3072]{1,0:T(8,128)(2,1)S(1)}, u32[]{:S(2)}, u32[]{:S(2)}) collective-permute-start(bf16[32,3072]{1,0:T(8,128)(2,1)S(1)} %get-tuple-element.46.refs_4_), channel_id=1, source_target_pairs={{0,2},{1,3},{2,0},{3,1},{4,6},{5,7},{6,4},{7,5},{8,10},{9,11},{10,... | collective-permute-start | bytes 589832 | tf_op jit(solution)/shard_map/ppermute | solution.py:23
  52.3 4.7 %collective-permute-start.9 = (bf16[64,3072]{1,0:T(8,128)(2,1)S(1)}, bf16[64,3072]{1,0:T(8,128)(2,1)S(1)}, u32[]{:S(2)}, u32[]{:S(2)}) collective-permute-start(bf16[64,3072]{1,0:T(8,128)(2,1)S(1)} %pad_maximum_fusion.2), channel_id=1, source_target_pairs={{0,1},{1,0},{2,3},{3,2},{4,5},{5,4},{6,7},{7,6},{8,9},{9,8},{10,11... | collective-permute-start | bytes 1179656 | tf_op jit(solution)/shard_map/ppermute | solution.py:23
  56.9 3.4 %collective-permute-start.13 = (bf16[32,3072]{1,0:T(8,128)(2,1)S(1)}, bf16[32,3072]{1,0:T(8,128)(2,1)S(1)}, u32[]{:S(2)}, u32[]{:S(2)}) collective-permute-start(bf16[32,3072]{1,0:T(8,128)(2,1)S(1)} %multiply_convert_fusion.refs_1_), channel_id=1, source_target_pairs={{0,1},{1,0},{2,3},{3,2},{4,5},{5,4},{6,7},{7,6},{8,9},{9,8},{10,11... | collective-permute-start | bytes 589832 | tf_op jit(solution)/shard_map/ppermute | solution.py:23
  59.7 7.8 %collective-permute-start.11 = (bf16[32,3072]{1,0:T(8,128)(2,1)S(1)}, bf16[32,3072]{1,0:T(8,128)(2,1)S(1)}, u32[]{:S(2)}, u32[]{:S(2)}) collective-permute-start(bf16[32,3072]{1,0:T(8,128)(2,1)S(1)} %get-tuple-element.38.refs_4_), channel_id=1, source_target_pairs={{0,4},{4,0},{8,12},{12,8},{16,20},{20,16},{24,28},{28,24},{1,5},{5... | collective-permute-start | bytes 589832 | tf_op jit(solution)/shard_map/ppermute | solution.py:23
  65.9 7.1 %collective-permute-start.14 = (bf16[32,3072]{1,0:T(8,128)(2,1)S(1)}, bf16[32,3072]{1,0:T(8,128)(2,1)S(1)}, u32[]{:S(2)}, u32[]{:S(2)}) collective-permute-start(bf16[32,3072]{1,0:T(8,128)(2,1)S(1)} %get-tuple-element.42.refs_2_), channel_id=1, source_target_pairs={{0,4},{4,0},{8,12},{12,8},{16,20},{20,16},{24,28},{28,24},{1,5},{5... | collective-permute-start | bytes 589832 | tf_op jit(solution)/shard_map/ppermute | solution.py:23
  73.1 7.0 %collective-permute-start.15 = (bf16[16,6144]{1,0:T(8,128)(2,1)S(1)}, bf16[16,6144]{1,0:T(8,128)(2,1)S(1)}, u32[]{:S(2)}, u32[]{:S(2)}) collective-permute-start(bf16[16,6144]{1,0:T(8,128)(2,1)S(1)} %fusion.6.refs_5_), channel_id=1, source_target_pairs={{0,8},{4,12},{8,0},{12,4},{16,24},{20,28},{24,16},{28,20},{1,9},{5... | collective-permute-start | bytes 589832 | tf_op jit(solution)/shard_map/ppermute | solution.py:23
  80.1 12.6 %collective-permute-start.16 = (bf16[8,6144]{1,0:T(8,128)(2,1)S(1)}, bf16[8,6144]{1,0:T(8,128)(2,1)S(1)}, u32[]{:S(2)}, u32[]{:S(2)}) collective-permute-start(bf16[8,6144]{1,0:T(8,128)(2,1)S(1)} %slice.179.refs_3_), channel_id=1, source_target_pairs={{0,16},{4,20},{8,24},{12,28},{16,0},{20,4},{24,8},{28,12},{1,17},{... | collective-permute-start | bytes 294920 | tf_op jit(solution)/shard_map/ppermute | solution.py:23

commit v5 on v4

--- a/solution.py
+++ b/solution.py
@@ -310,21 +310,20 @@
     n = left.shape[1]
     half = n // 2
     left, right = left.reshape(3 * n, h), right.reshape(3 * n, h)
+    part = w_in.shape[0] // 4
+    w_out_here = load(w_out, None, 0, part, ready[-3])
+    w_out_here = load(w_out, w_out_here, part, 3 * part, ready[-2], 6)
     w_in_here = load(w_in, None, 0, w_in.shape[0], ready[-1], 8)
-    part = w_out.shape[0] // 2
-    w_out_here = load(w_out, None, 0, part, ready[-3])
-    w_out_here = load(w_out, w_out_here, part, part, ready[-2])
     mine, send, w_in_here = into(me, left, right, w_in_here, (0, 2 * n, 2), NN, True, BF16)
     pre = pair_sum(mine, send)
-    sent = lax.optimization_barrier((pre[:half].astype(BF16), pre[half:].astype(BF16)))
-    mine, send, w_out_here = into(me, left, right, w_out_here, (2 * n, n, 1), NT, True, F32, sent[0])
+    sent = col_send(pre)
+    mine, send, w_out_here = into(me, left, right, w_out_here, (2 * n, n, 1), NT, True, F32, sent)
     back = pair_sum(mine, send)
     back_sent = col_send(back)
-    past = col_sum(pre[half:], sent[1])
-    act, slope = gelu_parts(past)
-    act, slope = lax.optimization_barrier((act.astype(BF16), slope))
-    now = col_sum(pre[:half], sent[0])
-    hidden = gelu_parts(now)[0].astype(BF16)
+    pre = col_sum(pre, sent)
+    act, slope = gelu_parts(pre[half:])
+    hidden = gelu_parts(pre[:half])[0].astype(BF16)
+    act = act.astype(BF16)
     own, slope = lax.optimization_barrier((jnp.concatenate([hidden, act], axis=0), slope))
     other = swap(own, "col", 1)
     layer = outof(me, own[:half], other[:half], w_out_here, NN, True, back_sent)
@@ -338,7 +337,7 @@
     sums = [keep + swap(send, "row", row_bits[0]).astype(F32) for (keep, send) in (layer, inp)]
     act_all, hidden_grad = in_order(low, own[half:], other[half:]), in_order(low, own_grad, other_grad)
     units = act_all.shape[1], past_all.shape[1]
-    share = units[0] * 2 // 3 // 128 * 128, units[1] // 3 // 128 * 128
+    share = units[0] * 3 // 4 // 128 * 128, units[1] * 3 // 8 // 128 * 128
     (grad_w_out,) = outer([(act_all, grad_all, None, 0, share[0])], inp[1])
     res = jnp.concatenate(sums, axis=1)
     for i, bit in enumerate(row_bits[1:]):

time: 93.6 us -> 97.3 us (1.040)
  starting transfers between devices: 18.5 us -> 21 us
  waiting for transfers between devices: 25.3 us -> 26.6 us
    ppermute x17 -> x16, starting transfers between devices: 18.5 us -> 21 us  [swap(): return lax.ppermute(x, axis, [(i, i ^ bit) for i in range(n)])]
    ppermute x17 -> x16, waiting for transfers between devices: 25.3 us -> 26.6 us  [swap(): return lax.ppermute(x, axis, [(i, i ^ bit) for i in range(n)])]
  transfers between devices with their start and end apart: 17 -> 16, of which waited for: 8 -> 6; matrix products, arithmetic and copies ran while one was open for 1% -> 1% of each run, Pallas kernels for 46% -> 39%
where the time goes in v5:
time: 97.3 us; the launch traced here: 97.1 us
  Pallas kernels  45.8 us (47%)
  waiting for transfers between devices  26.6 us (27%)
  starting transfers between devices  21 us (22%)
  other arithmetic  1.92 us (2%)
  between operations  1 us (1%)
    pallas_call x10, Pallas kernels, call(): pl.pallas_call(body, in_specs=in_specs, out_specs=out_specs, out_shape=ou...  45.8 us
    ppermute x16, waiting for transfers between devices, swap(): return lax.ppermute(x, axis, [(i, i ^ bit) for i in range(n)])  26.6 us
    ppermute x16, starting transfers between devices, swap(): return lax.ppermute(x, axis, [(i, i ^ bit) for i in range(n)])  21 us
  transfers between devices with their start and end apart: 16, of which 6 were waited for; matrix products, arithmetic and copies ran while one was open for 1% of the time, Pallas kernels for 39%

profile of v5, /device:TPU:0, one launch (start us, length us, event | category | flops | bytes accessed | tf_op | source)
XLA Modules:
  0.0 97.1 jit_solution(6749467141033102423)
XLA Ops:
  0.6 0.9 pad_maximum_fusion.9
  1.5 3.0 %collective-permute-start.3 = (bf16[3,8,1536]{2,1,0:T(8,128)(2,1)S(1)}, bf16[3,8,1536]{2,1,0:T(8,128)(2,1)S(1)}, u32[]{:S(2)}, u32[]{:S(2)}) collective-permute-start(bf16[3,8,1536]{2,1,0:T(8,128)(2,1)S(1)} %get-tuple-element.53.refs_1_), channel_id=1, source_target_pairs={{0,4},{4,0},{8,12},{12,8},{16,20},{20,16},{24,28},{28,24},{1,5},{5... | collective-permute-start | bytes 221192 | tf_op jit(solution)/shard_map/ppermute | solution.py:23
  4.6 2.6 %collective-permute-start = (bf16[3,8,1536]{2,1,0:T(8,128)(2,1)S(1)}, bf16[3,8,1536]{2,1,0:T(8,128)(2,1)S(1)}, u32[]{:S(2)}, u32[]{:S(2)}) collective-permute-start(bf16[3,8,1536]{2,1,0:T(8,128)(2,1)S(1)} %get-tuple-element.55), channel_id=1, source_target_pairs={{0,16},{4,20},{8,24},{12,28},{16,0},{20,4},{24,8},{28,12},{1,17},{... | collective-permute-start | bytes 221192 | tf_op jit(solution)/shard_map/ppermute | solution.py:23
  7.2 2.4 %shard_map.86.refs_1_ = bf16[3072,3072]{1,0:T(8,128)(2,1)S(1)} custom-call(bf16[3072,3072]{1,0:T(8,128)(2,1)} %refs_0_.5, bf16[3,8,1536]{2,1,0:T(8,128)(2,1)S(1)} %get-tuple-element.53.refs_1_), custom_call_target="tpu_custom_call" | custom-call | flops 301989888 | bytes 4718592 | tf_op jit(solution)/shard_map/pallas_call | solution.py:47
  9.6 0.5 collective-permute-start.4
  10.1 0.9 collective-permute-done
  11.0 3.2 %collective-permute-start.1 = (bf16[3,16,1536]{2,1,0:T(8,128)(2,1)S(1)}, bf16[3,16,1536]{2,1,0:T(8,128)(2,1)S(1)}, u32[]{:S(2)}, u32[]{:S(2)}) collective-permute-start(bf16[3,16,1536]{2,1,0:T(8,128)(2,1)S(1)} %pad_maximum_fusion.10), channel_id=1, source_target_pairs={{0,8},{4,12},{8,0},{12,4},{16,24},{20,28},{24,16},{28,20},{1,9},{5... | collective-permute-start | bytes 442376 | tf_op jit(solution)/shard_map/ppermute | solution.py:23
  14.2 5.2 %shard_map.87.refs_3_ = bf16[3072,3072]{1,0:T(8,128)(2,1)S(1)} custom-call(bf16[3072,3072]{1,0:T(8,128)(2,1)} %refs_0_.5, bf16[3072,3072]{1,0:T(8,128)(2,1)S(1)} %shard_map.86.refs_1_, bf16[3,16,1536]{2,1,0:T(8,128)(2,1)S(1)} %pad_maximum_fusion.11.refs_2_), custom_call_target="tpu_custom_call", output_to_operand_aliasing={{}: (1, {})} | custom-call | flops 905969664 | bytes 14155776 | tf_op jit(solution)/shard_map/pallas_call | solution.py:47
  19.5 0.1 collective-permute-start.5
  19.5 6.5 %shard_map.84.w_ref = bf16[3072,3072]{1,0:T(8,128)(2,1)S(1)} custom-call(bf16[3072,3072]{1,0:T(8,128)(2,1)} %refs_0_.3, bf16[3,32,1536]{2,1,0:T(8,128)(2,1)S(1)} %pad_maximum_fusion.8.refs_1_), custom_call_target="tpu_custom_call" | custom-call | flops 1207959552 | bytes 18874368 | tf_op jit(solution)/shard_map/pallas_call | solution.py:47
  26.3 6.6 %collective-permute-done.2 = bf16[3,32,1536]{2,1,0:T(8,128)(2,1)S(1)} collective-permute-done((bf16[3,32,1536]{2,1,0:T(8,128)(2,1)S(1)}, bf16[3,32,1536]{2,1,0:T(8,128)(2,1)S(1)}, u32[]{:S(2)}, u32[]{:S(2)}) %collective-permute-start.2) | collective-permute-done | bytes 294944 | tf_op jit(solution)/shard_map/ppermute | solution.py:23
  32.9 2.8 %shard_map.85 = (f32[64,3072]{1,0:T(8,128)S(1)}, bf16[64,3072]{1,0:T(8,128)(2,1)S(1)}, bf16[3072,3072]{1,0:T(8,128)(2,1)S(1)}) custom-call(s32[1]{0:T(128)} %bitcast.3.core_ref.refs_0_, bf16[192,1536]{1,0:T(8,128)(2,1)S(1)} %bitcast.14, bf16[192,1536]{1,0:T(8,128)(2,1)S(1)} %bitcast.16, ...), custom_call_target="tpu_custom_call", output_to_operand_aliasing={{2}: (3, {})} | custom-call | flops 1207959552 | bytes 18874368 | tf_op jit(solution)/shard_map/pallas_call | solution.py:47
  35.8 1.7 %collective-permute-done.6 = bf16[64,3072]{1,0:T(8,128)(2,1)S(1)} collective-permute-done((bf16[64,3072]{1,0:T(8,128)(2,1)S(1)}, bf16[64,3072]{1,0:T(8,128)(2,1)S(1)}, u32[]{:S(2)}, u32[]{:S(2)}) %collective-permute-start.6) | collective-permute-done | bytes 393248 | tf_op jit(solution)/shard_map/ppermute | solution.py:23
  37.6 5.4 %shard_map.88 = (f32[32,3072]{1,0:T(8,128)S(1)}, f32[32,3072]{1,0:T(8,128)S(1)}, bf16[3072,3072]{1,0:T(8,128)(2,1)S(1)}) custom-call(s32[1]{0:T(128)} %bitcast.3.core_ref.refs_0_, bf16[192,1536]{1,0:T(8,128)(2,1)S(1)} %bitcast.15, bf16[192,1536]{1,0:T(8,128)(2,1)S(1)} %bitcast.17, ...), custom_call_target="tpu_custom_call", output_to_operand_aliasing={{2}: (3, {})} | custom-call | flops 1207959552 | bytes 18874368 | tf_op jit(solution)/shard_map/pallas_call | solution.py:47
  42.9 0.2 collective-permute-start.9
  43.2 1.6 %collective-permute-start.7 = (bf16[64,3072]{1,0:T(8,128)(2,1)S(1)}, bf16[64,3072]{1,0:T(8,128)(2,1)S(1)}, u32[]{:S(2)}, u32[]{:S(2)}) collective-permute-start(bf16[64,3072]{1,0:T(8,128)(2,1)S(1)} %fusion.refs_4_), channel_id=1, source_target_pairs={{0,2},{1,3},{2,0},{3,1},{4,6},{5,7},{6,4},{7,5},{8,10},{9,11},{10,... | collective-permute-start | bytes 1179656 | tf_op jit(solution)/shard_map/ppermute | solution.py:23
  44.9 1.5 %collective-permute-start.11 = (bf16[32,3072]{1,0:T(8,128)(2,1)S(1)}, bf16[32,3072]{1,0:T(8,128)(2,1)S(1)}, u32[]{:S(2)}, u32[]{:S(2)}) collective-permute-start(bf16[32,3072]{1,0:T(8,128)(2,1)S(1)} %get-tuple-element.38.refs_4_), channel_id=1, source_target_pairs={{0,2},{1,3},{2,0},{3,1},{4,6},{5,7},{6,4},{7,5},{8,10},{9,11},{10,... | collective-permute-start | bytes 589832 | tf_op jit(solution)/shard_map/ppermute | solution.py:23
  46.4 8.9 %collective-permute-done.7 = bf16[64,3072]{1,0:T(8,128)(2,1)S(1)} collective-permute-done((bf16[64,3072]{1,0:T(8,128)(2,1)S(1)}, bf16[64,3072]{1,0:T(8,128)(2,1)S(1)}, u32[]{:S(2)}, u32[]{:S(2)}) %collective-permute-start.7) | collective-permute-done | bytes 393248 | tf_op jit(solution)/shard_map/ppermute | solution.py:23
  55.3 0.1 convert_add_fusion
  55.4 0.2 fusion.4
  55.7 3.1 %collective-permute-done.11 = bf16[32,3072]{1,0:T(8,128)(2,1)S(1)} collective-permute-done((bf16[32,3072]{1,0:T(8,128)(2,1)S(1)}, bf16[32,3072]{1,0:T(8,128)(2,1)S(1)}, u32[]{:S(2)}, u32[]{:S(2)}) %collective-permute-start.11) | collective-permute-done | bytes 196640 | tf_op jit(solution)/shard_map/ppermute | solution.py:23
  59.1 2.7 %shard_map.89 = (f32[32,3072]{1,0:T(8,128)S(1)}, bf16[32,3072]{1,0:T(8,128)(2,1)S(1)}) custom-call(s32[1]{0:T(128)} %bitcast.3.core_ref.refs_0_, bf16[32,3072]{1,0:T(8,128)(2,1)S(1)} %get-tuple-element.49.refs_1_, bf16[32,3072]{1,0:T(8,128)(2,1)S(1)} %get-tuple-element.50.refs_2_, bf16[3072,3072]{1,0:T(8,128)(2,1)S(1)} %get-tuple-element.26.refs_3_, ...), custom_call_target="tpu_custom_call" | custom-call | flops 1207959552 | bytes 18874368 | tf_op jit(solution)/shard_map/pallas_call | solution.py:47
  61.8 0.6 collective-permute-start.10
  62.4 5.6 %shard_map.90 = (f32[32,3072]{1,0:T(8,128)S(1)}, bf16[32,3072]{1,0:T(8,128)(2,1)S(1)}) custom-call(s32[1]{0:T(128)} %bitcast.3.core_ref.refs_0_, bf16[32,3072]{1,0:T(8,128)(2,1)S(1)} %multiply_convert_fusion.refs_1_, bf16[32,3072]{1,0:T(8,128)(2,1)S(1)} %collective-permute-done.12.refs_2_, bf16[3072,3072]{1,0:T(8,128)(2,1)S(1)} %get-tuple-element.32.refs_3_, ...), custom_call_target="tpu_custom_call" | custom-call | flops 1207959552 | bytes 18874368 | tf_op jit(solution)/shard_map/pallas_call | solution.py:47
  67.9 1.6 %collective-permute-start.13 = (bf16[32,3072]{1,0:T(8,128)(2,1)S(1)}, bf16[32,3072]{1,0:T(8,128)(2,1)S(1)}, u32[]{:S(2)}, u32[]{:S(2)}) collective-permute-start(bf16[32,3072]{1,0:T(8,128)(2,1)S(1)} %get-tuple-element.34.refs_2_), channel_id=1, source_target_pairs={{0,4},{4,0},{8,12},{12,8},{16,20},{20,16},{24,28},{28,24},{1,5},{5... | collective-permute-start | bytes 589832 | tf_op jit(solution)/shard_map/ppermute | solution.py:23
  69.6 5.4 %collective-permute-done.13 = bf16[32,3072]{1,0:T(8,128)(2,1)S(1)} collective-permute-done((bf16[32,3072]{1,0:T(8,128)(2,1)S(1)}, bf16[32,3072]{1,0:T(8,128)(2,1)S(1)}, u32[]{:S(2)}, u32[]{:S(2)}) %collective-permute-start.13) | collective-permute-done | bytes 196640 | tf_op jit(solution)/shard_map/ppermute | solution.py:23
  75.1 1.8 %collective-permute-start.14 = (bf16[16,6144]{1,0:T(8,128)(2,1)S(1)}, bf16[16,6144]{1,0:T(8,128)(2,1)S(1)}, u32[]{:S(2)}, u32[]{:S(2)}) collective-permute-start(bf16[16,6144]{1,0:T(8,128)(2,1)S(1)} %fusion.7.refs_5_), channel_id=1, source_target_pairs={{0,8},{4,12},{8,0},{12,4},{16,24},{20,28},{24,16},{28,20},{1,9},{5... | collective-permute-start | bytes 589832 | tf_op jit(solution)/shard_map/ppermute | solution.py:23
  77.0 5.6 %shard_map.91.refs_4_ = bf16[3072,3072]{1,0:T(8,128)(2,1)} custom-call(bf16[64,3072]{1,0:T(8,128)(2,1)S(1)} %pad_maximum_fusion.5.refs_0_, bf16[64,3072]{1,0:T(8,128)(2,1)S(1)} %pad_maximum_fusion.6.refs_1_, bf16[32,3072]{1,0:T(8,128)(2,1)S(1)} %get-tuple-element.34.refs_2_), custom_call_target="tpu_custom_call" | custom-call | flops 905969664 | bytes 14155776 | tf_op jit(solution)/shard_map/pallas_call | solution.py:47
  82.7 4.0 %collective-permute-start.15 = (bf16[8,6144]{1,0:T(8,128)(2,1)S(1)}, bf16[8,6144]{1,0:T(8,128)(2,1)S(1)}, u32[]{:S(2)}, u32[]{:S(2)}) collective-permute-start(bf16[8,6144]{1,0:T(8,128)(2,1)S(1)} %slice.169.refs_3_), channel_id=1, source_target_pairs={{0,16},{4,20},{8,24},{12,28},{16,0},{20,4},{24,8},{28,12},{1,17},{... | collective-permute-start | bytes 294920 | tf_op jit(solution)/shard_map/ppermute | solution.py:23
  86.6 4.9 %shard_map.92 = (bf16[3072,3072]{1,0:T(8,128)(2,1)}, bf16[3072,3072]{1,0:T(8,128)(2,1)}) custom-call(bf16[64,3072]{1,0:T(8,128)(2,1)S(1)} %pad_maximum_fusion.5.refs_0_, bf16[64,3072]{1,0:T(8,128)(2,1)S(1)} %pad_maximum_fusion.6.refs_1_, bf16[64,3072]{1,0:T(8,128)(2,1)S(1)} %get-tuple-element.58.refs_2_.refs_0_, ...), custom_call_target="tpu_custom_call", output_to_operand_aliasing={{0}: (4, {})} | custom-call | flops 754974720 | bytes 11796480 | tf_op jit(solution)/shard_map/pallas_call | solution.py:47
  91.6 4.8 %shard_map.93 = bf16[3072,3072]{1,0:T(8,128)(2,1)} custom-call(bf16[64,3072]{1,0:T(8,128)(2,1)S(1)} %get-tuple-element.58.refs_2_.refs_0_, bf16[64,3072]{1,0:T(8,128)(2,1)S(1)} %get-tuple-element.59.refs_3_.refs_1_, bf16[3072,3072]{1,0:T(8,128)(2,1)} %get-tuple-element.36.refs_2_, bf16[8,6144]{1,0:T(8,128)(2,1)S(1)} %slice.169.refs_3_), custom_call_target="tpu_custom_call", output_to_operand_aliasing={{}: (2, {})} | custom-call | flops 754974720 | bytes 11796480 | tf_op jit(solution)/shard_map/pallas_call | solution.py:47
  96.5 0.6 fusion.11
  (44 shorter events, 1.2 us)
Async XLA Ops:
  1.5 8.0 %collective-permute-start.3 = (bf16[3,8,1536]{2,1,0:T(8,128)(2,1)S(1)}, bf16[3,8,1536]{2,1,0:T(8,128)(2,1)S(1)}, u32[]{:S(2)}, u32[]{:S(2)}) collective-permute-start(bf16[3,8,1536]{2,1,0:T(8,128)(2,1)S(1)} %get-tuple-element.53.refs_1_), channel_id=1, source_target_pairs={{0,4},{4,0},{8,12},{12,8},{16,20},{20,16},{24,28},{28,24},{1,5},{5... | collective-permute-start | bytes 221192 | tf_op jit(solution)/shard_map/ppermute | solution.py:23
  4.6 6.4 %collective-permute-start = (bf16[3,8,1536]{2,1,0:T(8,128)(2,1)S(1)}, bf16[3,8,1536]{2,1,0:T(8,128)(2,1)S(1)}, u32[]{:S(2)}, u32[]{:S(2)}) collective-permute-start(bf16[3,8,1536]{2,1,0:T(8,128)(2,1)S(1)} %get-tuple-element.55), channel_id=1, source_target_pairs={{0,16},{4,20},{8,24},{12,28},{16,0},{20,4},{24,8},{28,12},{1,17},{... | collective-permute-start | bytes 221192 | tf_op jit(solution)/shard_map/ppermute | solution.py:23
  9.6 9.9 %collective-permute-start.4 = (bf16[3,16,1536]{2,1,0:T(8,128)(2,1)S(1)}, bf16[3,16,1536]{2,1,0:T(8,128)(2,1)S(1)}, u32[]{:S(2)}, u32[]{:S(2)}) collective-permute-start(bf16[3,16,1536]{2,1,0:T(8,128)(2,1)S(1)} %pad_maximum_fusion.11.refs_2_), channel_id=1, source_target_pairs={{0,16},{4,20},{8,24},{12,28},{16,0},{20,4},{24,8},{28,12},{1,17},{... | collective-permute-start | bytes 442376 | tf_op jit(solution)/shard_map/ppermute | solution.py:23
  11.0 15.1 %collective-permute-start.1 = (bf16[3,16,1536]{2,1,0:T(8,128)(2,1)S(1)}, bf16[3,16,1536]{2,1,0:T(8,128)(2,1)S(1)}, u32[]{:S(2)}, u32[]{:S(2)}) collective-permute-start(bf16[3,16,1536]{2,1,0:T(8,128)(2,1)S(1)} %pad_maximum_fusion.10), channel_id=1, source_target_pairs={{0,8},{4,12},{8,0},{12,4},{16,24},{20,28},{24,16},{28,20},{1,9},{5... | collective-permute-start | bytes 442376 | tf_op jit(solution)/shard_map/ppermute | solution.py:23
  19.5 6.8 %collective-permute-start.5 = (bf16[3,32,1536]{2,1,0:T(8,128)(2,1)S(1)}, bf16[3,32,1536]{2,1,0:T(8,128)(2,1)S(1)}, u32[]{:S(2)}, u32[]{:S(2)}) collective-permute-start(bf16[3,32,1536]{2,1,0:T(8,128)(2,1)S(1)} %pad_maximum_fusion.8.refs_1_), channel_id=1, source_target_pairs={{0,8},{4,12},{8,0},{12,4},{16,24},{20,28},{24,16},{28,20},{1,9},{5... | collective-permute-start | bytes 884744 | tf_op jit(solution)/shard_map/ppermute | solution.py:23
  26.1 6.8 %collective-permute-start.2 = (bf16[3,32,1536]{2,1,0:T(8,128)(2,1)S(1)}, bf16[3,32,1536]{2,1,0:T(8,128)(2,1)S(1)}, u32[]{:S(2)}, u32[]{:S(2)}) collective-permute-start(bf16[3,32,1536]{2,1,0:T(8,128)(2,1)S(1)} %pad_maximum_fusion.7), channel_id=1, source_target_pairs={{0,4},{4,0},{8,12},{12,8},{16,20},{20,16},{24,28},{28,24},{1,5},{5... | collective-permute-start | bytes 884744 | tf_op jit(solution)/shard_map/ppermute | solution.py:23
  35.7 1.8 %collective-permute-start.6 = (bf16[64,3072]{1,0:T(8,128)(2,1)S(1)}, bf16[64,3072]{1,0:T(8,128)(2,1)S(1)}, u32[]{:S(2)}, u32[]{:S(2)}) collective-permute-start(bf16[64,3072]{1,0:T(8,128)(2,1)S(1)} %get-tuple-element.24), channel_id=1, source_target_pairs={{0,1},{1,0},{2,3},{3,2},{4,5},{5,4},{6,7},{7,6},{8,9},{9,8},{10,11... | collective-permute-start | bytes 1179656 | tf_op jit(solution)/shard_map/ppermute | solution.py:23
  42.9 1.9 %collective-permute-start.9 = (f32[32,3072]{1,0:T(8,128)S(1)}, f32[32,3072]{1,0:T(8,128)S(1)}, u32[]{:S(2)}, u32[]{:S(2)}) collective-permute-start(f32[32,3072]{1,0:T(8,128)S(1)} %get-tuple-element.28), channel_id=1, source_target_pairs={{0,1},{1,0},{2,3},{3,2},{4,5},{5,4},{6,7},{7,6},{8,9},{9,8},{10,11... | collective-permute-start | bytes 1179656 | tf_op jit(solution)/shard_map/ppermute | solution.py:23
  43.2 12.1 %collective-permute-start.7 = (bf16[64,3072]{1,0:T(8,128)(2,1)S(1)}, bf16[64,3072]{1,0:T(8,128)(2,1)S(1)}, u32[]{:S(2)}, u32[]{:S(2)}) collective-permute-start(bf16[64,3072]{1,0:T(8,128)(2,1)S(1)} %fusion.refs_4_), channel_id=1, source_target_pairs={{0,2},{1,3},{2,0},{3,1},{4,6},{5,7},{6,4},{7,5},{8,10},{9,11},{10,... | collective-permute-start | bytes 1179656 | tf_op jit(solution)/shard_map/ppermute | solution.py:23
  44.9 14.0 %collective-permute-start.11 = (bf16[32,3072]{1,0:T(8,128)(2,1)S(1)}, bf16[32,3072]{1,0:T(8,128)(2,1)S(1)}, u32[]{:S(2)}, u32[]{:S(2)}) collective-permute-start(bf16[32,3072]{1,0:T(8,128)(2,1)S(1)} %get-tuple-element.38.refs_4_), channel_id=1, source_target_pairs={{0,2},{1,3},{2,0},{3,1},{4,6},{5,7},{6,4},{7,5},{8,10},{9,11},{10,... | collective-permute-start | bytes 589832 | tf_op jit(solution)/shard_map/ppermute | solution.py:23
  55.6 3.4 %collective-permute-start.8 = (bf16[64,3072]{1,0:T(8,128)(2,1)S(1)}, bf16[64,3072]{1,0:T(8,128)(2,1)S(1)}, u32[]{:S(2)}, u32[]{:S(2)}) collective-permute-start(bf16[64,3072]{1,0:T(8,128)(2,1)S(1)} %pad_maximum_fusion.2), channel_id=1, source_target_pairs={{0,1},{1,0},{2,3},{3,2},{4,5},{5,4},{6,7},{7,6},{8,9},{9,8},{10,11... | collective-permute-start | bytes 1179656 | tf_op jit(solution)/shard_map/ppermute | solution.py:23
  59.0 3.4 %collective-permute-start.12 = (bf16[32,3072]{1,0:T(8,128)(2,1)S(1)}, bf16[32,3072]{1,0:T(8,128)(2,1)S(1)}, u32[]{:S(2)}, u32[]{:S(2)}) collective-permute-start(bf16[32,3072]{1,0:T(8,128)(2,1)S(1)} %multiply_convert_fusion.refs_1_), channel_id=1, source_target_pairs={{0,1},{1,0},{2,3},{3,2},{4,5},{5,4},{6,7},{7,6},{8,9},{9,8},{10,11... | collective-permute-start | bytes 589832 | tf_op jit(solution)/shard_map/ppermute | solution.py:23
  61.8 13.3 %collective-permute-start.10 = (bf16[32,3072]{1,0:T(8,128)(2,1)S(1)}, bf16[32,3072]{1,0:T(8,128)(2,1)S(1)}, u32[]{:S(2)}, u32[]{:S(2)}) collective-permute-start(bf16[32,3072]{1,0:T(8,128)(2,1)S(1)} %get-tuple-element.30.refs_4_), channel_id=1, source_target_pairs={{0,4},{4,0},{8,12},{12,8},{16,20},{20,16},{24,28},{28,24},{1,5},{5... | collective-permute-start | bytes 589832 | tf_op jit(solution)/shard_map/ppermute | solution.py:23
  67.9 7.1 %collective-permute-start.13 = (bf16[32,3072]{1,0:T(8,128)(2,1)S(1)}, bf16[32,3072]{1,0:T(8,128)(2,1)S(1)}, u32[]{:S(2)}, u32[]{:S(2)}) collective-permute-start(bf16[32,3072]{1,0:T(8,128)(2,1)S(1)} %get-tuple-element.34.refs_2_), channel_id=1, source_target_pairs={{0,4},{4,0},{8,12},{12,8},{16,20},{20,16},{24,28},{28,24},{1,5},{5... | collective-permute-start | bytes 589832 | tf_op jit(solution)/shard_map/ppermute | solution.py:23
  75.1 7.5 %collective-permute-start.14 = (bf16[16,6144]{1,0:T(8,128)(2,1)S(1)}, bf16[16,6144]{1,0:T(8,128)(2,1)S(1)}, u32[]{:S(2)}, u32[]{:S(2)}) collective-permute-start(bf16[16,6144]{1,0:T(8,128)(2,1)S(1)} %fusion.7.refs_5_), channel_id=1, source_target_pairs={{0,8},{4,12},{8,0},{12,4},{16,24},{20,28},{24,16},{28,20},{1,9},{5... | collective-permute-start | bytes 589832 | tf_op jit(solution)/shard_map/ppermute | solution.py:23
  82.7 13.7 %collective-permute-start.15 = (bf16[8,6144]{1,0:T(8,128)(2,1)S(1)}, bf16[8,6144]{1,0:T(8,128)(2,1)S(1)}, u32[]{:S(2)}, u32[]{:S(2)}) collective-permute-start(bf16[8,6144]{1,0:T(8,128)(2,1)S(1)} %slice.169.refs_3_), channel_id=1, source_target_pairs={{0,16},{4,20},{8,24},{12,28},{16,0},{20,4},{24,8},{28,12},{1,17},{... | collective-permute-start | bytes 294920 | tf_op jit(solution)/shard_map/ppermute | solution.py:23
